TPU v7x, 256 devices: a whole 4x4x8 slice. The times are simulated.
256 devices in a mesh: seq: 64 (over z, y, core), head: 4 (over x).
Axes of the slice: x: 4, y: 4, z: 8, core: 2. Of those that a mesh axis runs over, the one named last changes fastest.
Arguments:
- inputs: bfloat16 [16384, 5120], P('seq', 'head'), may hold values from -6 to 6
- time_step: float32 [80, 16384], P('head', 'seq'), may hold values from 0.01 to 0.3
- decay_rate: float32 [80], P('head'), may hold values from 0.0001 to 1
- input_map: bfloat16 [16384, 128], P('seq'), may hold values from -6 to 6
- output_map: bfloat16 [16384, 128], P('seq'), may hold values from -0.59765625 to 0.59765625
- output_grad: bfloat16 [16384, 5120], P('seq', 'head'), may hold values from -3 to 3
- span_states: float32 [64, 80, 64, 128], P('seq', 'head'), may hold values from -6 to 6
- resets: int32 [64], P('seq'), may hold values from 0 to 4095
Outputs:
- grad_inputs: bfloat16 [16384, 5120], P('seq', 'head')
- grad_input_map: float32 [16384, 128], P('seq')
- grad_rate: float32 [80], P('head')
Inputs may be any that keep to these rules, and one draw needn't show every extreme that they name: `resets`: A value p under 256 means that a document starts at position p of that span; a value of 256 or more means that none starts in it.
All inputs are finite; a program needn't handle non-finite values.
Results may differ from a plain program's by a relative error of at most 0.003.
Values sent between devices are 32-bit elements; how exact they have to be, the bound alone decides.
No kernel may reach another device: no remote copies, remote signals or barrier semaphores. Data moves between devices by JAX's collectives and lax.ppermute only.
A program may use at most 64 MiB of HBM per device.

v0:
```python
import jax
import jax.numpy as jnp
from jax import lax
from jax.sharding import Mesh
from jax.sharding import PartitionSpec as P

SEQ = ("seq_0", "seq_1", "seq_2")


highest = lax.Precision.HIGHEST


def in_blocks(array, dim, devices):
    dims = array.shape
    pieces = array.reshape(*dims[:dim], devices, dims[dim] // devices, *dims[dim + 1 :])
    return jnp.moveaxis(pieces, dim, 0)


def laid_out(pieces, dim):
    pieces = jnp.moveaxis(pieces, 0, dim)
    dims = pieces.shape
    return pieces.reshape(*dims[:dim], dims[dim] * dims[dim + 1], *dims[dim + 2 :])


def moved_by_axis(pieces, axes, sequence):
    inside = pieces.shape[1:]
    filled = pieces.reshape(*(lax.axis_size(a) for a in axes), *inside)
    for k in sequence:
        filled = lax.all_to_all(filled, axes[k], k, k, tiled=True)
    return filled.reshape(-1, *inside)


def exchange_by_chip(array, groups, sequence, split_dim, concat_dim):
    devices = lax.axis_size(groups[0]) * lax.axis_size(groups[1])
    pieces = in_blocks(array, split_dim, devices)
    return laid_out(moved_by_axis(pieces, groups, sequence), concat_dim)


def sent_to_all(array, axis):
    copies = jnp.broadcast_to(array, (lax.axis_size(axis), *array.shape))
    return lax.all_to_all(copies, axis, split_axis=0, concat_axis=0, tiled=True)


def gather_directly(array, axis, dim):
    pieces = sent_to_all(array, axis)
    return laid_out(pieces, dim)


def of_everyone(array, axis):
    everything = sent_to_all(array, axis)
    return jnp.sum(everything, axis=0)


def prepare(x_block, step_block, decay_rate, b_block, c_block, grad_block, start_state, reset_at):
    block_len = step_block.shape[1]
    positions = jnp.arange(block_len, dtype=jnp.int32)
    later_doc = positions >= reset_at
    no_reset = reset_at >= block_len
    elapsed = jnp.cumsum(step_block, axis=1)
    log_decay = -decay_rate[:, None] * elapsed
    joined = (later_doc[:, None] == later_doc[None, :]) & (positions[None, :] >= positions[:, None])
    log_gaps = log_decay[:, None, :] - log_decay[:, :, None]
    pair_weight = jnp.where(joined[None], jnp.exp(jnp.where(joined[None], log_gaps, 0.0)), 0.0)
    intersection = jnp.dot(b_block, c_block.T, preferred_element_type=jnp.float32)
    products = jnp.einsum("shp,uhp->hsu", x_block, grad_block, preferred_element_type=jnp.float32)
    mixing = (pair_weight * intersection[None]).astype(jnp.bfloat16)
    pair_terms = pair_weight * products
    paired = pair_terms.astype(jnp.bfloat16)
    dx_inner = jnp.einsum("hsu,uhp->shp", mixing, grad_block, preferred_element_type=jnp.float32)
    db_inner = jnp.einsum("hsu,un->hsn", paired, c_block, preferred_element_type=jnp.float32)
    start_weight = jnp.where(later_doc[None], 0.0, jnp.exp(log_decay))
    end_weight = jnp.where(
        (later_doc | no_reset)[None], jnp.exp(log_decay[:, -1:] - log_decay), 0.0
    )
    carry_gain = jnp.where(no_reset, jnp.exp(log_decay[:, -1]), 0.0)
    c_wide = c_block.astype(jnp.float32)
    grad_wide = grad_block.astype(jnp.float32)
    weighted_c = start_weight[:, :, None] * c_wide[None]
    boundary_grad = jnp.einsum("hun,uhp->hpn", weighted_c, grad_wide, precision=highest)
    state_read = jnp.einsum("uhp,hpn->hun", grad_wide, start_state, precision=highest)
    start_term = jnp.sum(state_read * c_wide[None], axis=2)
    inside_term = jnp.sum(
        pair_terms
        * intersection[None]
        * step_block[:, :, None]
        * (elapsed[:, None, :] - elapsed[:, :, None]),
        axis=(1, 2),
    )
    entry_term = jnp.sum(start_weight * elapsed * start_term, axis=1)
    return (
        carry_gain,
        boundary_grad,
        dx_inner,
        db_inner,
        inside_term + entry_term,
        end_weight,
        elapsed,
    )


def finish(prepared, x_block, step_block, b_block, start_state, carried):
    carry_gain, boundary_grad, dx_inner, db_inner, partial_rate, end_weight, elapsed = prepared
    b_wide = b_block.astype(jnp.float32)
    x_wide = x_block.astype(jnp.float32)
    carried_b = jnp.einsum("sn,hpn->shp", b_wide, carried, precision=highest)
    carried_x = jnp.einsum("shp,hpn->hsn", x_wide, carried, precision=highest)
    step_rows = step_block.T[:, :, None]
    end_rows = end_weight.T[:, :, None]
    grad_x = (step_rows * (dx_inner + end_rows * carried_b)).astype(jnp.bfloat16)
    grad_b = jnp.sum(
        step_block[:, :, None] * (db_inner + end_weight[:, :, None] * carried_x), axis=0
    )
    last_elapsed = elapsed[:, -1]
    leaving_term = jnp.sum(
        end_weight
        * step_block
        * (last_elapsed[:, None] - elapsed)
        * jnp.sum(carried_x * b_wide[None], axis=2),
        axis=1,
    )
    through_term = carry_gain * last_elapsed * jnp.sum(carried * start_state, axis=(1, 2))
    return (grad_x, grad_b, partial_rate + leaving_term + through_term)


def backward_step(running, members):
    grad_piece, gain_piece = members
    return (grad_piece + gain_piece[:, None] * running, running)


def body(inputs, time_step, decay_rate, input_map, output_map, output_grad, span_states, resets):
    length = time_step.shape[1]
    block_count = span_states.shape[0]
    block_len = length // block_count
    head_count = decay_rate.shape[0]
    head_width = inputs.shape[1] // head_count
    number = 0
    x_block = inputs.reshape(block_len, head_count, head_width)
    grad_block = output_grad.reshape(block_len, head_count, head_width)
    step_block = time_step
    b_block = input_map
    prepared = prepare(
        x_block,
        step_block,
        decay_rate,
        b_block,
        output_map,
        grad_block,
        span_states[number],
        resets[number],
    )
    pieces = [(prepared, x_block, step_block, b_block)]
    gain_total = jnp.ones((head_count,), jnp.float32)
    grad_total = jnp.zeros_like(span_states[0])
    for number in reversed(range(block_count)):
        gain_block, grad_block_sum = (pieces[number][0][0], pieces[number][0][1])
        grad_total = grad_block_sum + gain_block[:, None, None] * grad_total
        gain_total = gain_block * gain_total
    received = exchange_by_chip(grad_total, (("seq_0", "seq_1"), "seq_2"), (0, 1), 1, 1)
    gains = gather_directly(gain_total[None], SEQ, 0)
    ending, exclusive = lax.scan(
        backward_step,
        jnp.zeros_like(received[:, 0]),
        (jnp.transpose(received, (1, 0, 2)), gains),
        reverse=True,
    )
    returned = lax.all_to_all(
        jnp.transpose(exclusive, (1, 0, 2)), SEQ, split_axis=1, concat_axis=1, tiled=True
    )
    carried = returned
    grad_x_list = [None] * block_count
    grad_b_list = [None] * block_count
    rate_total = jnp.zeros((head_count,), jnp.float32)
    for number in reversed(range(block_count)):
        prepared, x_block, step_block, b_block = pieces[number]
        grad_x, grad_b, rate_part = finish(
            prepared, x_block, step_block, b_block, span_states[number], carried
        )
        grad_x_list[number] = grad_x.reshape(block_len, head_count * head_width)
        grad_b_list[number] = grad_b
        rate_total = rate_part
        carried = prepared[1] + prepared[0][:, None, None] * carried
    grad_inputs = grad_x_list[0]
    grad_input_map = of_everyone(grad_b_list[0], "head")
    grad_rate = -of_everyone(rate_total, SEQ)
    return (grad_inputs, grad_input_map, grad_rate)


def solution(mesh):
    split = Mesh(
        mesh.devices.reshape(8, 4, 2, mesh.shape["head"]), ("seq_0", "seq_1", "seq_2", "head")
    )
    placed = (
        P(SEQ, "head"),
        P("head", SEQ),
        P("head"),
        P(SEQ, None),
        P(SEQ, None),
        P(SEQ, "head"),
        P(SEQ, "head", None, None),
        P(SEQ),
    )
    return jax.shard_map(
        body,
        mesh=split,
        in_specs=placed,
        out_specs=(P(SEQ, "head"), P(SEQ, None), P("head")),
        check_vma=False,
    )
```

profile of v0, /device:TPU:1, one launch (start us, length us, event | category | flops | bytes accessed | tf_op | source)
XLA Modules:
  0.0 169.3 jit_solution(9818807428464444261)
XLA Ops:
  1.4 0.7 neg.7
  2.0 0.8 reshape.285
  4.0 0.9 copy.100
  5.0 1.4 copy.99
  6.4 1.8 %fusion.29 = f32[20,128,64]{1,2,0:T(8,128)S(1)} fusion(bf16[256,20,64]{0,2,1:T(8,128)(2,1)S(1)} %bitcast.94, f32[256,128]{0,1:T(8,128)S(1)} %copy.100, f32[20,256]{1,0:T(8,128)S(1)} %get-tuple-element.182, f32[20]{0:T(128)S(1)} %get-tuple-element.178), kind=kOutput, calls=%fused_computation.39 | convolution fusion | flops 504135680 | bytes 1462352 | tf_op jit(solution)/shard_map/hun,uhp->hpn/dot_general | solution.py:79
  8.2 1.1 copy.102
  9.3 12.2 %all-to-all-start = ((f32[32,2,20,1,128]{4,1,2,3,0:T(2,128)}), f32[32,2,20,1,128]{4,1,2,3,0:T(2,128)S(1)}, u32[]{:S(2)}, u32[]{:S(2)}) async-start(f32[32,2,20,1,128]{4,1,2,3,0:T(2,128)} %copy.102), calls=%async_computation | async-start | bytes 1310720 | tf_op jit(solution)/shard_map/all_to_all | solution.py:29
  21.6 18.5 %all-to-all-done = f32[32,2,20,1,128]{4,1,2,3,0:T(2,128)S(1)} async-done(((f32[32,2,20,1,128]{4,1,2,3,0:T(2,128)}), f32[32,2,20,1,128]{4,1,2,3,0:T(2,128)S(1)}, u32[]{:S(2)}, u32[]{:S(2)}) %all-to-all-start) | async-done | bytes 655392 | tf_op jit(solution)/shard_map/all_to_all | solution.py:29
  40.2 6.4 %all_to_all.31 = f32[32,2,20,1,128]{4,0,2,3,1:T(8,128)S(1)} all-to-all(f32[32,2,20,1,128]{4,0,2,3,1:T(8,128)S(1)} %copy.103), channel_id=1, replica_groups=mesh['seq_0'=8,'seq_1'=4,'seq_2'=2,'head'=4] {'seq_2'}, dimensions={1} | all-to-all | bytes 1310720 | tf_op jit(solution)/shard_map/all_to_all | solution.py:29
  46.6 0.6 broadcast_in_dim.107
  47.2 5.5 %all-to-all-start.2 = ((f32[64,1,20]{2,1,0:T(1,128)}), f32[64,1,20]{2,1,0:T(1,128)S(1)}, u32[]{:S(2)}, u32[]{:S(2)}) async-start(f32[64,1,20]{2,1,0:T(1,128)} %broadcast_in_dim.107), calls=%async_computation.2 | async-start | bytes 65536 | tf_op jit(solution)/shard_map/all_to_all | solution.py:41
  53.4 0.7 convert_element_type.21
  54.8 7.3 %all-to-all-done.2 = f32[64,1,20]{2,1,0:T(1,128)S(1)} async-done(((f32[64,1,20]{2,1,0:T(1,128)}), f32[64,1,20]{2,1,0:T(1,128)S(1)}, u32[]{:S(2)}, u32[]{:S(2)}) %all-to-all-start.2) | async-done | bytes 5152 | tf_op jit(solution)/shard_map/all_to_all | solution.py:41
  62.1 1.0 broadcast_in_dim.104
  63.1 45.2 %while.17 = (s32[]{:T(128)}, f32[20,128]{1,0:T(8,128)S(1)}, f32[64,20,128]{2,1,0:T(8,128)}, f32[64,20,128]{2,0,1:T(8,128)S(1)}, f32[64,20]{1,0:T(8,128)S(1)}, /*index=5*/s32[]{:T(128)}, s32[]{:T(128)}, s32[]{:T(128)}) while((s32[]{:T(128)}, f32[20,128]{1,0:T(8,128)S(1)}, f32[64,20,128]{2,1,0:T(8,128)}, ...), condition=%wide.region_3.4_spmd.clone, body=%wide.region_2.3_spmd.clone.sunk | while | flops 10244 | bytes 74096 | solution.py:160
  64.5 0.6 bitcast_dynamic-update-slice_fusion.2
  68.0 0.6 bitcast_dynamic-update-slice_fusion.2
  70.2 0.6 bitcast_dynamic-update-slice_fusion.2
  72.3 0.6 bitcast_dynamic-update-slice_fusion.2
  73.0 0.6 bitcast_dynamic-update-slice_fusion.2
  74.4 0.6 bitcast_dynamic-update-slice_fusion.2
  77.9 0.6 bitcast_dynamic-update-slice_fusion.2
  80.1 0.6 bitcast_dynamic-update-slice_fusion.2
  85.0 0.6 bitcast_dynamic-update-slice_fusion.2
  85.7 0.6 bitcast_dynamic-update-slice_fusion.2
  89.9 0.6 bitcast_dynamic-update-slice_fusion.2
  91.3 0.6 bitcast_dynamic-update-slice_fusion.2
  101.9 0.6 bitcast_dynamic-update-slice_fusion.2
  104.0 0.6 bitcast_dynamic-update-slice_fusion.2
  105.4 0.6 bitcast_dynamic-update-slice_fusion.2
  106.1 0.6 bitcast_dynamic-update-slice_fusion.2
  108.2 4.8 %all-to-all-start.3 = ((f32[20,64,128]{2,0,1:T(8,128)}), f32[20,64,128]{2,0,1:T(8,128)S(1)}, u32[]{:S(2)}, u32[]{:S(2)}) async-start(f32[20,64,128]{2,0,1:T(8,128)} %bitcast.14), calls=%async_computation.3 | async-start | bytes 1572864 | tf_op jit(solution)/shard_map/all_to_all | solution.py:166
  113.0 2.3 %multiply_reduce_fusion.1 = f32[20,256]{1,0:T(8,128)S(1)} fusion(bf16[256,20,64]{0,2,1:T(8,128)(2,1)S(1)} %bitcast.95, f32[256,128]{0,1:T(8,128)} %copy-done.8, f32[1,20,64,128]{3,2,1,0:T(8,128)S(1)} %copy-done.1), kind=kOutput, calls=%fused_computation.19 | convolution fusion | flops 504622080 | bytes 1462272 | tf_op jit(solution)/shard_map/uhp,hpn->hun/dot_general | solution.py:80
  115.4 1.0 fusion.45
  116.5 4.9 %multiply_reduce_fusion = (f32[20]{0:T(128)S(1)}, f32[20,256,256]{2,1,0:T(8,128)}) fusion(f32[20,256]{1,0:T(8,128)S(1)} %bitcast.101, f32[20,256]{1,0:T(8,128)S(1)} %copy-done.7, f32[256,256]{1,0:T(8,128)S(1)} %fusion.45, f32[20,256]{1,0:T(8,128)S(1)} %get-tuple-element.183, pred[256,256]{1,0:T(8,128)(4,1)S(1)} %fusion.39, ...), kind=kOutput, calls=%fused_computation.6 | convolution fusion | flops 179568624 | bytes 6942800 | tf_op jit(solution)/shard_map/shp,uhp->hsu/dot_general | solution.py:65
  121.4 14.8 %all-to-all-done.3 = f32[20,64,128]{2,0,1:T(8,128)S(1)} async-done(((f32[20,64,128]{2,0,1:T(8,128)}), f32[20,64,128]{2,0,1:T(8,128)S(1)}, u32[]{:S(2)}, u32[]{:S(2)}) %all-to-all-start.3) | async-done | bytes 655392 | tf_op jit(solution)/shard_map/all_to_all | solution.py:166
  136.2 2.8 %fusion.10 = (f32[20,256]{1,0:T(8,128)S(1)}, f32[20,128,256]{1,2,0:T(8,128)}) fusion(f32[256,128]{1,0:T(8,128)S(1)} %copy-done.3, bf16[256,20,64]{0,2,1:T(8,128)(2,1)S(1)} %bitcast.91, f32[20,64,128]{2,0,1:T(8,128)S(1)} %all-to-all-done.3), kind=kOutput, calls=%fused_computation.18 | convolution fusion | flops 504622080 | bytes 4083712 | tf_op jit(solution)/shard_map/shp,hpn->hsn/dot_general | solution.py:106
  139.7 0.6 broadcast_in_dim.111
  140.3 5.9 %all-to-all-start.5 = ((f32[64,1,20]{2,1,0:T(1,128)}), f32[64,1,20]{2,1,0:T(1,128)S(1)}, u32[]{:S(2)}, u32[]{:S(2)}) async-start(f32[64,1,20]{2,1,0:T(1,128)} %broadcast_in_dim.111), calls=%async_computation.5 | async-start | bytes 65536 | tf_op jit(solution)/shard_map/all_to_all | solution.py:41
  146.2 5.5 %fusion.9 = f32[256,128]{1,0:T(8,128)S(1)} fusion(f32[20,128,256]{1,2,0:T(8,128)} %get-tuple-element.185, f32[20,256]{1,0:T(8,128)S(1)} %get-tuple-element.180, f32[20,256]{1,0:T(8,128)S(1)} %copy-done.7, f32[20,256,256]{2,1,0:T(8,128)} %get-tuple-element.187, f32[20,256]{1,0:T(8,128)S(1)} %get-tuple-element.183, pred[256,256]{1,0:T(8,128)(4,1)S(1)} %fusion.39, ...), kind=kOutput, calls=%fused_computation.17 | convolution fusion | flops 344686592 | bytes 8187904 | tf_op jit(solution)/shard_map/hsu,un->hsn/dot_general | solution.py:70
  151.7 3.8 %all-to-all-done.5 = f32[64,1,20]{2,1,0:T(1,128)S(1)} async-done(((f32[64,1,20]{2,1,0:T(1,128)}), f32[64,1,20]{2,1,0:T(1,128)S(1)}, u32[]{:S(2)}, u32[]{:S(2)}) %all-to-all-start.5) | async-done | bytes 5152 | tf_op jit(solution)/shard_map/all_to_all | solution.py:41
  155.5 0.8 broadcast_in_dim.108
  156.3 4.0 %all-to-all-start.4 = ((f32[4,256,128]{2,1,0:T(8,128)}), f32[4,256,128]{2,1,0:T(8,128)S(1)}, u32[]{:S(2)}, u32[]{:S(2)}) async-start(f32[4,256,128]{2,1,0:T(8,128)} %broadcast_in_dim.108), calls=%async_computation.4 | async-start | bytes 1048576 | tf_op jit(solution)/shard_map/all_to_all | solution.py:41
  160.3 1.5 fusion.22
  161.8 0.7 fusion.26
  162.5 1.1 copy.113
  164.2 4.4 %all-to-all-done.4 = f32[4,256,128]{2,1,0:T(8,128)S(1)} async-done(((f32[4,256,128]{2,1,0:T(8,128)}), f32[4,256,128]{2,1,0:T(8,128)S(1)}, u32[]{:S(2)}, u32[]{:S(2)}) %all-to-all-start.4) | async-done | bytes 524320 | tf_op jit(solution)/shard_map/all_to_all | solution.py:41
  168.7 0.7 reduce_sum.82
  (298 shorter events, 39.3 us)
Async XLA Ops:
  0.6 52.7 %copy-start.2 = (bf16[256,128]{1,0:T(8,128)(2,1)S(1)}, bf16[256,128]{1,0:T(8,128)(2,1)}, u32[]{:S(2)}) copy-start(bf16[256,128]{1,0:T(8,128)(2,1)} %param.13) | copy-start | bytes 196612
  0.6 53.4 %copy-start = (bf16[256,1280]{1,0:T(8,128)(2,1)S(1)}, bf16[256,1280]{1,0:T(8,128)(2,1)}, u32[]{:S(2)}) copy-start(bf16[256,1280]{1,0:T(8,128)(2,1)} %param.10) | copy-start | bytes 1966084
  2.0 2.0 %copy-start.13 = (f32[20]{0:T(128)}, f32[20]{0:T(128)S(1)}, u32[]{:S(2)}) copy-start(f32[20]{0:T(128)S(1)} %neg.7) | copy-start | bytes 244
  4.0 2.4 %copy-start.9 = (f32[20]{0:T(128)}, f32[20]{0:T(128)S(1)}, u32[]{:S(2)}) copy-start(f32[20]{0:T(128)S(1)} %slice_reduce_fusion.2) | copy-start | bytes 244
  5.0 4.3 %copy-start.8 = (f32[256,128]{0,1:T(8,128)}, f32[256,128]{0,1:T(8,128)S(1)}, u32[]{:S(2)}) copy-start(f32[256,128]{0,1:T(8,128)S(1)} %copy.100) | copy-start | bytes 393220
  6.4 46.4 %copy-start.11 = (f32[20]{0:T(128)}, f32[20]{0:T(128)S(1)}, u32[]{:S(2)}) copy-start(f32[20]{0:T(128)S(1)} %get-tuple-element.179) | copy-start | bytes 244
  9.2 103.8 %copy-start.1 = (f32[1,20,64,128]{3,2,1,0:T(8,128)S(1)}, f32[1,20,64,128]{3,2,1,0:T(8,128)}, u32[]{:S(2)}) copy-start(f32[1,20,64,128]{3,2,1,0:T(8,128)} %param.16) | copy-start | bytes 1966084
  9.3 30.8 %all-to-all-start = ((f32[32,2,20,1,128]{4,1,2,3,0:T(2,128)}), f32[32,2,20,1,128]{4,1,2,3,0:T(2,128)S(1)}, u32[]{:S(2)}, u32[]{:S(2)}) async-start(f32[32,2,20,1,128]{4,1,2,3,0:T(2,128)} %copy.102), calls=%async_computation | async-start | bytes 1310720 | tf_op jit(solution)/shard_map/all_to_all | solution.py:29
  21.6 94.9 %copy-start.7 = (f32[20,256]{1,0:T(8,128)S(1)}, f32[20,256]{1,0:T(8,128)}, u32[]{:S(2)}) copy-start(f32[20,256]{1,0:T(8,128)} %param.11) | copy-start | bytes 61444
  47.2 14.9 %all-to-all-start.2 = ((f32[64,1,20]{2,1,0:T(1,128)}), f32[64,1,20]{2,1,0:T(1,128)S(1)}, u32[]{:S(2)}, u32[]{:S(2)}) async-start(f32[64,1,20]{2,1,0:T(1,128)} %broadcast_in_dim.107), calls=%async_computation.2 | async-start | bytes 65536 | tf_op jit(solution)/shard_map/all_to_all | solution.py:41
  108.2 27.9 %all-to-all-start.3 = ((f32[20,64,128]{2,0,1:T(8,128)}), f32[20,64,128]{2,0,1:T(8,128)S(1)}, u32[]{:S(2)}, u32[]{:S(2)}) async-start(f32[20,64,128]{2,0,1:T(8,128)} %bitcast.14), calls=%async_computation.3 | async-start | bytes 1572864 | tf_op jit(solution)/shard_map/all_to_all | solution.py:166
  116.5 4.9 %copy-start.4 = (f32[256,256]{1,0:T(8,128)}, f32[256,256]{1,0:T(8,128)S(1)}, u32[]{:S(2)}) copy-start(f32[256,256]{1,0:T(8,128)S(1)} %fusion.45) | copy-start | bytes 786436
  116.5 19.7 %copy-start.3 = (f32[256,128]{1,0:T(8,128)S(1)}, f32[256,128]{1,0:T(8,128)}, u32[]{:S(2)}) copy-start(f32[256,128]{1,0:T(8,128)} %convert_element_type.21) | copy-start | bytes 393220
  116.5 22.5 %copy-start.10 = (f32[20]{0:T(128)S(1)}, f32[20]{0:T(128)}, u32[]{:S(2)}) copy-start(f32[20]{0:T(128)} %copy-done.9) | copy-start | bytes 244
  116.5 22.5 %copy-start.14 = (f32[20]{0:T(128)S(1)}, f32[20]{0:T(128)}, u32[]{:S(2)}) copy-start(f32[20]{0:T(128)} %copy-done.13) | copy-start | bytes 244
  116.5 22.5 %copy-start.15 = (pred[256]{0:T(512)(128)(4,1)S(1)}, pred[256]{0:T(512)(128)(4,1)}, u32[]{:S(2)}) copy-start(pred[256]{0:T(512)(128)(4,1)} %broadcast_or_fusion) | copy-start | bytes 772
  121.4 18.3 %copy-start.12 = (f32[20]{0:T(128)S(1)}, f32[20]{0:T(128)}, u32[]{:S(2)}) copy-start(f32[20]{0:T(128)} %copy-done.11) | copy-start | bytes 244
  121.4 24.8 %copy-start.6 = (bf16[256,128]{1,0:T(8,128)(2,1)S(1)}, bf16[256,128]{1,0:T(8,128)(2,1)}, u32[]{:S(2)}) copy-start(bf16[256,128]{1,0:T(8,128)(2,1)} %param.14) | copy-start | bytes 196612
  140.3 15.2 %all-to-all-start.5 = ((f32[64,1,20]{2,1,0:T(1,128)}), f32[64,1,20]{2,1,0:T(1,128)S(1)}, u32[]{:S(2)}, u32[]{:S(2)}) async-start(f32[64,1,20]{2,1,0:T(1,128)} %broadcast_in_dim.111), calls=%async_computation.5 | async-start | bytes 65536 | tf_op jit(solution)/shard_map/all_to_all | solution.py:41
  146.2 14.2 %copy-start.5 = (f32[256,256]{1,0:T(8,128)S(1)}, f32[256,256]{1,0:T(8,128)}, u32[]{:S(2)}) copy-start(f32[256,256]{1,0:T(8,128)} %copy-done.4) | copy-start | bytes 786436
  156.3 12.3 %all-to-all-start.4 = ((f32[4,256,128]{2,1,0:T(8,128)}), f32[4,256,128]{2,1,0:T(8,128)S(1)}, u32[]{:S(2)}, u32[]{:S(2)}) async-start(f32[4,256,128]{2,1,0:T(8,128)} %broadcast_in_dim.108), calls=%async_computation.4 | async-start | bytes 1048576 | tf_op jit(solution)/shard_map/all_to_all | solution.py:41
where the time goes:
time: 170 us; the launch traced here: 169 us
  waiting for transfers between devices  48.8 us (29%)
  other arithmetic  48.2 us (28%)
  starting transfers between devices  32.3 us (19%)
  matrix products  20.5 us (12%)
  local copies, waits for them, and re-layouts  11.1 us (7%)
  blocking collectives  6.38 us (4%)
    dynamic_update_slice x64, other arithmetic, body(): lax.scan(backward_step, jnp.zeros_like(received[:, 0]), (jnp.transpose(re...  38.7 us
    all_to_all x1, waiting for transfers between devices, moved_by_axis(): filled = lax.all_to_all(filled, axes[k], k, k, tiled=True)  18.5 us
    all_to_all x3, waiting for transfers between devices, sent_to_all(): return lax.all_to_all(copies, axis, split_axis=0, concat_axis=0, tiled=True)  15.6 us
    all_to_all x3, starting transfers between devices, sent_to_all(): return lax.all_to_all(copies, axis, split_axis=0, concat_axis=0, tiled=True)  15.4 us
    all_to_all x1, waiting for transfers between devices, body(): lax.all_to_all(jnp.transpose(exclusive, (1, 0, 2)), SEQ, split_axis=1, co...  14.8 us
    all_to_all x1, starting transfers between devices, moved_by_axis(): filled = lax.all_to_all(filled, axes[k], k, k, tiled=True)  12.2 us
    all_to_all x1, blocking collectives, moved_by_axis(): filled = lax.all_to_all(filled, axes[k], k, k, tiled=True)  6.38 us
    dot_general x1, matrix products, prepare(): jnp.einsum('hsu,un->hsn', paired, c_block, preferred_element_type=jnp.flo...  5.45 us
  transfers between devices with their start and end apart: 5, of which 5 were waited for; matrix products, arithmetic and copies ran while one was open for 12% of the time, Pallas kernels for 0%

commit v1 on v0

v1 whole, which is shorter than its diff:
```python
import functools

import jax
import jax.numpy as jnp
from jax import lax
from jax.experimental import pallas as pl
from jax.experimental.pallas import tpu as pltpu
from jax.sharding import Mesh
from jax.sharding import PartitionSpec as P

CHIPS = ("seq_0", "seq_1")
CORE = "seq_2"
SEQ = CHIPS + (CORE,)
f32, bf16 = jnp.float32, jnp.bfloat16

HEADS, WIDTH, STATE, SPAN = 20, 64, 128, 256
COLS = HEADS * WIDTH
HALF = COLS // 2
CHUNK = 256
STEPS = COLS // CHUNK
SHARES = 32
MIDDLE = SPAN // 2 - 1

NN = (((1,), (0,)), ((), ()))
NT = (((1,), (1,)), ((), ()))
TN = (((0,), (0,)), ((), ()))


def dot(a, b, dims):
    return lax.dot_general(a, b, dims, preferred_element_type=f32)


def two_parts(a):
    high = a.astype(bf16)
    return high, (a - high.astype(f32)).astype(bf16)


def three_parts(a):
    high = a.astype(bf16)
    rest = a - high.astype(f32)
    mid = rest.astype(bf16)
    return high, mid, (rest - mid.astype(f32)).astype(bf16)


def dot3(a, b, dims):
    return dot(a[0], b[0], dims) + (dot(a[0], b[1], dims) + dot(a[1], b[0], dims))


def iota(shape, dim):
    return lax.broadcasted_iota(jnp.int32, shape, dim)


def spread(chunk):
    shape = (128, CHUNK)
    lane = iota(shape, 0)
    head = (iota(shape, 1) + chunk * CHUNK) >> 6
    return jnp.where(((lane & 31) == head) & (lane < 96), 1.0, 0.0).astype(bf16)


def packed(a):
    high, mid, low = three_parts(a)
    lane = iota(a.shape, 1)
    return jnp.where(
        lane < 32, high.astype(f32), jnp.where(lane < 64, mid.astype(f32), low.astype(f32))
    ).astype(bf16)


def small_factors(rate_ref, step_ref, pad_ref, with_steps):
    pad_ref[...] = jnp.zeros_like(pad_ref)
    for copy in range(3):
        pad_ref[32 * copy : 32 * copy + HEADS, :] = step_ref[...]
    parts = three_parts(pad_ref[...])
    row, col = iota((SPAN, SPAN), 0), iota((SPAN, SPAN), 1)
    lower = jnp.where(col <= row, 1.0, 0.0).astype(bf16)
    elapsed = dot(lower, parts[0], NT) + (dot(lower, parts[1], NT) + dot(lower, parts[2], NT))
    lane = iota((1, 128), 1) & 31
    rate = jnp.zeros((1, 128), f32)
    for h in range(HEADS):
        rate = jnp.where(lane == h, rate_ref[h], rate)
    log_decay = -rate * elapsed
    if not with_steps:
        return elapsed, log_decay, None
    same = jnp.where(col == row, 1.0, 0.0).astype(bf16)
    steps = (dot(same, parts[0], NT) + dot(same, parts[1], NT)) + dot(same, parts[2], NT)
    return elapsed, log_decay, steps


def boundary_kernel(
    reset_ref, core_ref, rate_ref, step_ref, c_ref, grad_ref, keep_ref, send_ref, pad_ref, all_ref
):
    reset, core = reset_ref[0], core_ref[0]
    elapsed, log_decay, _ = small_factors(rate_ref, step_ref, pad_ref, False)
    later = iota((SPAN, 128), 0) >= reset
    weight = packed(jnp.where(later, 0.0, jnp.exp(log_decay)))
    gain = jnp.where(reset >= SPAN, jnp.exp(log_decay[SPAN - 1 :, :]), 0.0)
    gain = packed(jnp.broadcast_to(gain, (8, 128)))
    for chunk in range(STEPS):
        cols = pl.ds(chunk * CHUNK, CHUNK)
        wide = spread(chunk)
        weighted = dot(weight, wide, NN) * grad_ref[:, cols].astype(f32)
        high, low = two_parts(weighted)
        all_ref[:STATE, cols] = dot(c_ref[...], high, TN) + dot(c_ref[...], low, TN)
        all_ref[STATE:, cols] = dot(gain, wide, NN)
    keep_ref[...] = all_ref[:, pl.ds(pl.multiple_of(core * HALF, HALF), HALF)]
    send_ref[...] = all_ref[:, pl.ds(pl.multiple_of((1 - core) * HALF, HALF), HALF)]


def combine_kernel(core_ref, keep_ref, got_ref, out_ref):
    first = core_ref[0] == 0
    upper = iota((STATE, 128), 0) & 7

    def tile(t):
        cols = slice(128 * t, 128 * t + 128)
        keep, got = keep_ref[:, cols], got_ref[:, cols]
        early, late = jnp.where(first, keep, got), jnp.where(first, got, keep)
        early_gain, late_gain = early[STATE : STATE + 1], late[STATE : STATE + 1]
        return early[:STATE] + early_gain * late[:STATE], early_gain * late_gain

    tiles = [tile(t) for t in range(5)]
    for b in range(2):
        (one, one_gain), (two, two_gain), (last, last_gain) = tiles[2 * b], tiles[2 * b + 1], tiles[4]
        out_ref[b, :, 0:8, :] = one.reshape(16, 8, 128)
        out_ref[b, :, 8:16, :] = two.reshape(16, 8, 128)
        if b == 1:
            last = pltpu.roll(last, STATE - 4, 0)
        last = jnp.where(upper < 4, last, jnp.where(upper == 4, one_gain, jnp.where(upper == 5, two_gain, last_gain)))
        out_ref[b, :, 16:24, :] = last.reshape(16, 8, 128)


def scan_kernel(in_ref, out_ref):
    rows = iota((8, 128), 0)
    run = [jnp.zeros((8, 128), f32) for _ in range(3)]
    for k in reversed(range(SHARES)):
        tail = in_ref[k, 16:24, :]
        pieces = (in_ref[k, 0:8, :], in_ref[k, 8:16, :], jnp.where(rows < 4, tail, 0.0))
        for i in range(3):
            out_ref[k, 8 * i : 8 * i + 8, :] = run[i]
            run[i] = pieces[i] + tail[4 + i : 5 + i] * run[i]


def return_kernel(core_ref, back_ref, keep_ref, got_ref, mine_ref, send_ref):
    first = core_ref[0] == 0
    upper = iota((STATE, 128), 0) & 7
    for t in range(5):
        cols = slice(128 * t, 128 * t + 128)
        if t < 4:
            entering = back_ref[t // 2, :, 8 * (t % 2) : 8 * (t % 2) + 8, :].reshape(STATE, 128)
        else:
            low = back_ref[0, :, 16:24, :].reshape(STATE, 128)
            high = back_ref[1, :, 16:24, :].reshape(STATE, 128)
            entering = jnp.where(upper < 4, low, pltpu.roll(high, 4, 0))
        late = jnp.where(first, got_ref[:, cols], keep_ref[:, cols])
        passed = late[:STATE] + late[STATE : STATE + 1] * entering
        mine_ref[:, cols] = jnp.where(first, passed, entering)
        send_ref[:, cols] = jnp.where(first, entering, passed)


def local_kernel(
    reset_ref,
    rate_ref,
    step_ref,
    b_ref,
    c_ref,
    x_ref,
    grad_ref,
    state_ref,
    inner_ref,
    factor_ref,
    high_ref,
    low_ref,
    inner_b_ref,
    mate_ref,
    rate_out_ref,
    pad_ref,
    pairs_ref,
):
    reset = reset_ref[0]
    elapsed, log_decay, steps = small_factors(rate_ref, step_ref, pad_ref, True)
    later = iota((SPAN, 128), 0) >= reset
    no_reset = reset >= SPAN
    middle = log_decay[MIDDLE : MIDDLE + 1, :]
    last_log, last_elapsed = log_decay[SPAN - 1 :, :], elapsed[SPAN - 1 :, :]
    centred = log_decay - middle
    up = packed(jnp.exp(centred))
    down = packed(steps * jnp.exp(-centred))
    end = jnp.where(later | no_reset, jnp.exp(last_log - log_decay), 0.0)
    end_steps = packed(steps * end)
    elapsed_parts = packed(elapsed)
    rows = jnp.concatenate(
        [
            jnp.exp(middle),
            jnp.where(no_reset, jnp.exp(last_log), 0.0) * last_elapsed,
            last_elapsed,
            jnp.zeros((5, 128), f32),
        ],
        axis=0,
    )
    rows = packed(rows)
    row, col = iota((SPAN, SPAN), 0), iota((SPAN, SPAN), 1)
    joined = (col >= row) & ((row >= reset) == (col >= reset))
    b, c = b_ref[...], c_ref[...]
    masked = two_parts(jnp.where(joined, dot(b, c, NT), 0.0))
    c_start = jnp.where(later, 0.0, c.astype(f32)).astype(bf16)
    pairs_ref[...] = jnp.zeros_like(pairs_ref)
    rate_out_ref[...] = jnp.zeros_like(rate_out_ref)

    def step(chunk, carry):
        cols = pl.ds(pl.multiple_of(chunk * CHUNK, CHUNK), CHUNK)
        wide = spread(chunk)
        wide_rows = dot(rows, wide, NN)
        x, grad = x_ref[:, cols].astype(f32), grad_ref[:, cols].astype(f32)
        wide_elapsed = dot(elapsed_parts, wide, NN)
        scaled_grad = dot(up, wide, NN) * grad
        grad_parts = two_parts(scaled_grad)
        aged_parts = two_parts(wide_elapsed * scaled_grad)
        wide_down = dot(down, wide, NN)
        scaled_x = wide_down * x
        pairs_ref[...] += dot3(two_parts(scaled_x), grad_parts, NT)
        plain = dot3(masked, grad_parts, NN)
        aged = dot3(masked, aged_parts, NN)
        inner_ref[:, cols] = wide_down * plain
        inside = jnp.sum(scaled_x * (aged - wide_elapsed * plain), axis=0, keepdims=True)
        state = jnp.transpose(state_ref[cols, :])
        start = dot(c_start, aged_parts[0], TN) + dot(c_start, aged_parts[1], TN)
        entry = wide_rows[0:1] * jnp.sum(state * start, axis=0, keepdims=True)
        factor = dot(end_steps, wide, NN)
        factor_ref[:, cols] = factor
        leaving = factor * x
        high, low = two_parts(leaving)
        high_ref[:, cols] = high
        low_ref[:, cols] = low
        left = two_parts(leaving * (wide_rows[2:3] - wide_elapsed))
        mate_ref[:, cols] = dot(b, left[0], TN) + dot(b, left[1], TN) + wide_rows[1:2] * state
        totals = three_parts(jnp.broadcast_to(inside + entry, (8, CHUNK)))
        rate_out_ref[...] += dot(totals[0], wide, NT) + (
            dot(totals[1], wide, NT) + dot(totals[2], wide, NT)
        )
        return carry

    lax.fori_loop(0, STEPS, step, 0)
    pairs = two_parts(jnp.where(joined, pairs_ref[...], 0.0))
    inner_b_ref[...] = dot(pairs[0], c, NN) + dot(pairs[1], c, NN)


def reduce_kernel(
    core_ref, mine_ref, other_ref, high_ref, low_ref, inner_b_ref, mate_ref, rate_ref,
    all_ref, grad_b_ref, rate_out_ref,
):
    core = core_ref[0]
    all_ref[:, pl.ds(pl.multiple_of(core * HALF, HALF), HALF)] = mine_ref[...]
    all_ref[:, pl.ds(pl.multiple_of((1 - core) * HALF, HALF), HALF)] = other_ref[...]
    total = inner_b_ref[...]
    rate = rate_ref[...]
    for chunk in range(STEPS):
        cols = pl.ds(chunk * CHUNK, CHUNK)
        carried = all_ref[:, cols]
        total += dot3((high_ref[:, cols], low_ref[:, cols]), two_parts(carried), NT)
        sums = jnp.sum(carried * mate_ref[:, cols], axis=0, keepdims=True)
        sums = three_parts(jnp.broadcast_to(sums, (8, CHUNK)))
        wide = spread(chunk)
        rate += dot(sums[0], wide, NT) + (dot(sums[1], wide, NT) + dot(sums[2], wide, NT))
    for i in range(4):
        grad_b_ref[i] = total
    for i in range(64):
        rate_out_ref[i] = rate[0:1]


def inputs_kernel(b_ref, all_ref, inner_ref, factor_ref, out_ref):
    b = b_ref[...]
    for chunk in range(STEPS):
        cols = pl.ds(chunk * CHUNK, CHUNK)
        high, low = two_parts(all_ref[:, cols])
        product = dot(b, high, NN) + dot(b, low, NN)
        out_ref[:, cols] = (inner_ref[:, cols] + factor_ref[:, cols] * product).astype(bf16)


SMEM = pl.BlockSpec(memory_space=pltpu.SMEM)
VMEM = pl.BlockSpec(memory_space=pltpu.VMEM)
ANY = pl.BlockSpec(memory_space=pl.ANY)


def call(
    kernel, name, smem, args, outs, scratch=(), flops=1_000_000, size=1_000_000, after=(), grant=8
):
    def run(*refs):
        kernel(*refs[: len(args)], *refs[len(args) + len(after) :])

    return pl.pallas_call(
        run,
        name=name,
        in_specs=[SMEM] * smem + [VMEM] * (len(args) - smem) + [ANY] * len(after),
        out_specs=[VMEM] * len(outs),
        out_shape=[jax.ShapeDtypeStruct(shape, dtype) for shape, dtype in outs],
        scratch_shapes=[pltpu.VMEM(shape, dtype) for shape, dtype in scratch],
        cost_estimate=pl.CostEstimate(flops=flops, bytes_accessed=size, transcendentals=0),
        compiler_params=pltpu.CompilerParams(vmem_limit_bytes=grant << 20),
    )(*args, *after)


def body(inputs, time_step, decay_rate, input_map, output_map, output_grad, span_states, resets):
    core = lax.axis_index(CORE).astype(jnp.int32).reshape(1)
    states = span_states.reshape(COLS, STATE)
    swap = [(0, 1), (1, 0)]
    keep, send = call(
        boundary_kernel, "boundary", 3,
        (resets, core, decay_rate, time_step, output_map, output_grad),
        [((STATE + 8, HALF), f32)] * 2,
        [((128, SPAN), f32), ((STATE + 8, COLS), f32)],
    )
    got = lax.ppermute(send, CORE, swap)
    (pieces,) = call(combine_kernel, "combine", 1, (core, keep, got), [((2, 16, 24, 128), f32)])
    received = lax.all_to_all(pieces.reshape(SHARES, 24, 128), CHIPS, 0, 0, tiled=True)
    inner, factor, high, low, inner_b, mate, rate_local = call(
        local_kernel, "local", 2,
        (resets, decay_rate, time_step, input_map, output_map, inputs, output_grad, states),
        [
            ((SPAN, COLS), f32), ((SPAN, COLS), f32), ((SPAN, COLS), bf16), ((SPAN, COLS), bf16),
            ((SPAN, STATE), f32), ((STATE, COLS), f32), ((8, 128), f32),
        ],
        [((128, SPAN), f32), ((SPAN, SPAN), f32)],
        flops=6_000_000_000, size=8_000_000, after=(pieces,), grant=16,
    )
    (exclusive,) = call(scan_kernel, "carry", 0, (received,), [((SHARES, 24, 128), f32)], after=(rate_local,))
    back = lax.all_to_all(exclusive, CHIPS, 0, 0, tiled=True)
    mine, onward = call(
        return_kernel, "spread", 1, (core, back.reshape(2, 16, 24, 128), keep, got),
        [((STATE, HALF), f32)] * 2,
    )
    other = lax.ppermute(onward, CORE, swap)
    carried, grad_b, rate = call(
        reduce_kernel, "reduce", 1, (core, mine, other, high, low, inner_b, mate, rate_local),
        [((STATE, COLS), f32), ((4, SPAN, STATE), f32), ((64, 1, 128), f32)],
    )
    rates = lax.all_to_all(rate, SEQ, 0, 0, tiled=True)
    grad_bs = lax.all_to_all(grad_b, "head", 0, 0, tiled=True)
    (grad_inputs,) = call(
        inputs_kernel, "inputs", 0, (input_map, carried, inner, factor), [((SPAN, COLS), bf16)],
        flops=2_000_000_000, size=4_000_000,
    )
    grad_rate = -jnp.sum(rates[:, 0, :HEADS], axis=0)
    return grad_inputs, jnp.sum(grad_bs, axis=0), grad_rate


def solution(mesh):
    split = Mesh(
        mesh.devices.reshape(8, 4, 2, mesh.shape["head"]), ("seq_0", "seq_1", "seq_2", "head")
    )
    placed = (
        P(SEQ, "head"),
        P("head", SEQ),
        P("head"),
        P(SEQ, None),
        P(SEQ, None),
        P(SEQ, "head"),
        P(SEQ, "head", None, None),
        P(SEQ),
    )
    return jax.shard_map(
        body,
        mesh=split,
        in_specs=placed,
        out_specs=(P(SEQ, "head"), P(SEQ, None), P("head")),
        check_vma=False,
    )
```

time: 170 us -> 89.1 us (0.52)
  other arithmetic: 48.2 us -> 1.28 us
  waiting for transfers between devices: 48.8 us -> 8.72 us
  blocking collectives: 6.38 us -> 34.4 us
  matrix products: 20.5 us -> 0 us
  starting transfers between devices: 32.3 us -> 19.5 us
  Pallas kernels: 0 us -> 12.1 us
    all_to_all x5 -> x2, waiting for transfers between devices: 48.8 us -> 6.18 us  [the longest x1 3.75 us: body(): grad_bs = lax.all_to_all(grad_b, 'head', 0, 0, tiled=True)]
    dynamic_update_slice x64 -> x0, other arithmetic: 38.7 us -> none  [body(): lax.scan(backward_step, jnp.zeros_like(received[:, 0]), (jnp.transpose(re...]
    all_to_all x1 -> x2, blocking collectives: 6.38 us -> 34.4 us  [the longest x1 20.5 us: body(): back = lax.all_to_all(exclusive, CHIPS, 0, 0, tiled=True)]
    dot_general x8 -> x0, matrix products: 20.5 us -> none  [the longest x1 5.45 us: prepare(): jnp.einsum('hsu,un->hsn', paired, c_block, preferred_element_type=jnp.flo...]
    all_to_all x5 -> x2, starting transfers between devices: 32.3 us -> 13.5 us  [the longest x1 9.5 us: body(): lax.all_to_all(pieces.reshape(SHARES, 24, 128), CHIPS, 0, 0, tiled=True)]
    pallas_call x0 -> x7, Pallas kernels: none -> 12.1 us  [call(): pl.pallas_call(run, name=name, in_specs=[SMEM] * smem + [VMEM] * (len(arg...]
    unnamed x37 -> x34, local copies, waits for them, and re-layouts: 2.77 us -> 11.1 us
    ppermute x0 -> x2, starting transfers between devices: none -> 5.95 us  [the longest x1 3.29 us: body(): got = lax.ppermute(send, CORE, swap)]
  transfers between devices with their start and end apart: 5 -> 4, of which waited for: 5 -> 4; matrix products, arithmetic and copies ran while one was open for 12% -> 1% of each run, Pallas kernels for 0% -> 9%
where the time goes in v1:
time: 89.1 us; the launch traced here: 88.5 us
  blocking collectives  34.4 us (39%)
  starting transfers between devices  19.5 us (22%)
  Pallas kernels  12.1 us (14%)
  local copies, waits for them, and re-layouts  11.1 us (12%)
  waiting for transfers between devices  8.72 us (10%)
  between operations  1.4 us (2%)
  other arithmetic  1.28 us (1%)
    all_to_all x1, blocking collectives, body(): back = lax.all_to_all(exclusive, CHIPS, 0, 0, tiled=True)  20.5 us
    all_to_all x1, blocking collectives, body(): rates = lax.all_to_all(rate, SEQ, 0, 0, tiled=True)  13.9 us
    pallas_call x7, Pallas kernels, call(): pl.pallas_call(run, name=name, in_specs=[SMEM] * smem + [VMEM] * (len(arg...  12.1 us
    unnamed x34, local copies, waits for them, and re-layouts  11.1 us
    all_to_all x1, starting transfers between devices, body(): lax.all_to_all(pieces.reshape(SHARES, 24, 128), CHIPS, 0, 0, tiled=True)  9.5 us
    all_to_all x1, starting transfers between devices, body(): grad_bs = lax.all_to_all(grad_b, 'head', 0, 0, tiled=True)  4.03 us
    all_to_all x1, waiting for transfers between devices, body(): grad_bs = lax.all_to_all(grad_b, 'head', 0, 0, tiled=True)  3.75 us
    ppermute x1, starting transfers between devices, body(): got = lax.ppermute(send, CORE, swap)  3.29 us
  transfers between devices with their start and end apart: 4, of which 4 were waited for; matrix products, arithmetic and copies ran while one was open for 1% of the time, Pallas kernels for 9%

profile of v1, /device:TPU:1, one launch (start us, length us, event | category | flops | bytes accessed | tf_op | source)
XLA Modules:
  0.0 88.5 jit_solution(18308865477017851922)
XLA Ops:
  1.3 0.0 copy-start
  1.3 1.1 %copy-done = bf16[256,1280]{1,0:T(8,128)(2,1)S(1)} copy-done((bf16[256,1280]{1,0:T(8,128)(2,1)S(1)}, bf16[256,1280]{1,0:T(8,128)(2,1)}, u32[]{:S(2)}) %copy-start) | copy-done | bytes 655384
  2.4 0.0 copy-start.4
  2.4 0.8 copy-done.4
  3.2 0.0 copy-start.6
  3.2 0.7 copy-done.6
  3.9 0.0 copy-start.8
  4.0 0.7 copy-done.8
  4.6 0.0 copy-start.1
  4.6 0.0 copy-start.5
  4.6 0.0 copy-start.7
  4.6 0.0 copy-start.9
  4.6 0.0 copy-start.12
  4.6 1.8 %boundary.1 = (f32[136,640]{1,0:T(8,128)S(1)}, f32[136,640]{1,0:T(8,128)S(1)}) custom-call(s32[1]{0:T(128)S(6)} %copy.11.refs_0_, s32[1]{0:T(128)} %bitcast.refs_1_.refs_0_, f32[20]{0:T(128)S(1)} %copy-done.8, f32[20,256]{1,0:T(8,128)S(1)} %copy-done.6, bf16[256,128]{1,0:T(8,128)(2,1)S(1)} %copy-done.4, bf16[256,1280]{1,0:T(8,128)(2,1)S(1)} %copy-done), custom_call_target="tpu_custom_call" | custom-call | flops 1000000 | bytes 1000000 | tf_op jit(solution)/shard_map/boundary/pallas_call | solution.py:288
  6.4 3.3 %collective-permute-start = (f32[136,640]{1,0:T(8,128)S(1)}, f32[136,640]{1,0:T(8,128)S(1)}, u32[]{:S(2)}, u32[]{:S(2)}) collective-permute-start(f32[136,640]{1,0:T(8,128)S(1)} %get-tuple-element.18), channel_id=1, source_target_pairs={{0,4},{4,0},{1,5},{5,1},{2,6},{6,2},{3,7},{7,3},{8,12},{12,8},{9,1... | collective-permute-start | bytes 1044488 | tf_op jit(solution)/shard_map/ppermute | solution.py:310
  9.7 1.3 %collective-permute-done.refs_2_.refs_3_ = f32[136,640]{1,0:T(8,128)S(1)} collective-permute-done((f32[136,640]{1,0:T(8,128)S(1)}, f32[136,640]{1,0:T(8,128)S(1)}, u32[]{:S(2)}, u32[]{:S(2)}) %collective-permute-start) | collective-permute-done | bytes 348192 | tf_op jit(solution)/shard_map/ppermute | solution.py:310
  11.0 0.9 combine.1.refs_8_
  11.8 9.5 %all-to-all-start = ((f32[32,24,128]{2,1,0:T(8,128)}), f32[32,24,128]{2,1,0:T(8,128)S(1)}, u32[]{:S(2)}, u32[]{:S(2)}) async-start(f32[32,24,128]{2,1,0:T(8,128)} %bitcast.1), calls=%async_computation | async-start | bytes 786432 | tf_op jit(solution)/shard_map/all_to_all | solution.py:312
  21.3 0.0 copy-done.1
  21.3 0.0 copy-done.5
  21.4 0.0 copy-done.7
  21.4 0.0 copy-done.9
  21.4 0.0 copy-done.12
  21.4 0.0 copy-start.10
  21.4 1.1 %copy-done.10 = bf16[256,1280]{1,0:T(8,128)(2,1)S(1)} copy-done((bf16[256,1280]{1,0:T(8,128)(2,1)S(1)}, bf16[256,1280]{1,0:T(8,128)(2,1)}, u32[]{:S(2)}) %copy-start.10) | copy-done | bytes 655384
  22.5 1.1 %copy-done.11 = f32[1,20,64,128]{3,2,1,0:T(8,128)S(1)} copy-done((f32[1,20,64,128]{3,2,1,0:T(8,128)S(1)}, f32[1,20,64,128]{3,2,1,0:T(8,128)}, u32[]{:S(2)}) %copy-start.11) | copy-done | bytes 655384
  23.6 6.2 %local.1 = (f32[256,1280]{1,0:T(8,128)S(1)}, f32[256,1280]{1,0:T(8,128)S(1)}, bf16[256,1280]{1,0:T(8,128)(2,1)S(1)}, bf16[256,1280]{1,0:T(8,128)(2,1)S(1)}, f32[...) custom-call(s32[1]{0:T(128)S(6)} %copy.11.refs_0_, f32[20]{0:T(128)S(1)} %copy-done.9, ...), custom_call_target="tpu_custom_call" | custom-call | flops 6000000000 | bytes 8000000 | tf_op jit(solution)/shard_map/local/pallas_call | solution.py:288
  29.8 0.0 copy-start.2
  29.8 0.8 copy-done.2
  30.6 1.1 %copy-done.13 = f32[256,1280]{1,0:T(8,128)} copy-done((f32[256,1280]{1,0:T(8,128)}, f32[256,1280]{1,0:T(8,128)S(1)}, u32[]{:S(2)}) %copy-start.13) | copy-done | bytes 1310744
  31.7 1.1 %copy-done.15 = f32[256,1280]{1,0:T(8,128)} copy-done((f32[256,1280]{1,0:T(8,128)}, f32[256,1280]{1,0:T(8,128)S(1)}, u32[]{:S(2)}) %copy-start.15) | copy-done | bytes 1310744
  32.8 2.4 %all-to-all-done.refs_0_ = f32[32,24,128]{2,1,0:T(8,128)S(1)} async-done(((f32[32,24,128]{2,1,0:T(8,128)}), f32[32,24,128]{2,1,0:T(8,128)S(1)}, u32[]{:S(2)}, u32[]{:S(2)}) %all-to-all-start) | async-done | bytes 393248 | tf_op jit(solution)/shard_map/all_to_all | solution.py:312
  35.2 0.1 carry.1
  35.3 20.5 %all_to_all.20 = f32[32,24,128]{2,1,0:T(8,128)S(1)} all-to-all(f32[32,24,128]{2,1,0:T(8,128)S(1)} %carry.1), channel_id=1, replica_groups=mesh['seq_0'=8,'seq_1'=4,'seq_2'=2,'head'=4] {'seq_0','seq_1'}, dimensions={0} | all-to-all | bytes 786432 | tf_op jit(solution)/shard_map/all_to_all | solution.py:324
  55.8 0.1 spread.1
  55.9 2.7 %collective-permute-start.1 = (f32[128,640]{1,0:T(8,128)S(1)}, f32[128,640]{1,0:T(8,128)S(1)}, u32[]{:S(2)}, u32[]{:S(2)}) collective-permute-start(f32[128,640]{1,0:T(8,128)S(1)} %get-tuple-element.21), channel_id=1, source_target_pairs={{0,4},{4,0},{1,5},{5,1},{2,6},{6,2},{3,7},{7,3},{8,12},{12,8},{9,1... | collective-permute-start | bytes 983048 | tf_op jit(solution)/shard_map/ppermute | solution.py:329
  58.5 1.3 %collective-permute-done.1.refs_2_ = f32[128,640]{1,0:T(8,128)S(1)} collective-permute-done((f32[128,640]{1,0:T(8,128)S(1)}, f32[128,640]{1,0:T(8,128)S(1)}, u32[]{:S(2)}, u32[]{:S(2)}) %collective-permute-start.1) | collective-permute-done | bytes 327712 | tf_op jit(solution)/shard_map/ppermute | solution.py:329
  59.8 0.0 copy-done.3
  59.8 1.7 %reduce.2 = (f32[128,1280]{1,0:T(8,128)S(1)}, f32[4,256,128]{2,1,0:T(8,128)}, f32[64,1,128]{2,1,0:T(1,128)S(1)}) custom-call(s32[1]{0:T(128)} %bitcast.refs_1_.refs_0_, f32[128,640]{1,0:T(8,128)S(1)} %get-tuple-element.20.refs_1_, f32[128,640]{1,0:T(8,128)S(1)} %collective-permute-done.1.refs_2_, bf16[256,1280]{1,0:T(8,128)(2,1)S(1)} %get-tuple-element.22.refs_3_, ...), custom_call_target="tpu_custom_call" | custom-call | flops 1000000 | bytes 1000000 | tf_op jit(solution)/shard_map/reduce/pallas_call | solution.py:288
  61.5 13.9 %all_to_all.21 = f32[64,1,128]{2,1,0:T(1,128)S(1)} all-to-all(f32[64,1,128]{2,1,0:T(1,128)S(1)} %get-tuple-element.30), channel_id=1, replica_groups=mesh['seq_0'=8,'seq_1'=4,'seq_2'=2,'head'=4] {'seq_0','seq_1','seq_2'}, dimensions={0} | all-to-all | bytes 65536 | tf_op jit(solution)/shard_map/all_to_all | solution.py:334
  75.5 4.0 %all-to-all-start.2 = ((f32[4,256,128]{2,1,0:T(8,128)}), f32[4,256,128]{2,1,0:T(8,128)S(1)}, u32[]{:S(2)}, u32[]{:S(2)}) async-start(f32[4,256,128]{2,1,0:T(8,128)} %get-tuple-element.29), calls=%async_computation.2 | async-start | bytes 1048576 | tf_op jit(solution)/shard_map/all_to_all | solution.py:335
  79.5 1.3 %copy-done.14 = f32[256,1280]{1,0:T(8,128)S(1)} copy-done((f32[256,1280]{1,0:T(8,128)S(1)}, f32[256,1280]{1,0:T(8,128)}, u32[]{:S(2)}) %copy-start.14) | copy-done | bytes 1310744
  80.8 1.3 %copy-done.16 = f32[256,1280]{1,0:T(8,128)S(1)} copy-done((f32[256,1280]{1,0:T(8,128)S(1)}, f32[256,1280]{1,0:T(8,128)}, u32[]{:S(2)}) %copy-start.16) | copy-done | bytes 1310744
  82.1 1.3 %inputs.1 = bf16[256,1280]{1,0:T(8,128)(2,1)} custom-call(bf16[256,128]{1,0:T(8,128)(2,1)S(1)} %copy-done.12, f32[128,1280]{1,0:T(8,128)S(1)} %get-tuple-element.26.refs_1_, f32[256,1280]{1,0:T(8,128)S(1)} %copy-done.14, f32[256,1280]{1,0:T(8,128)S(1)} %copy-done.16), custom_call_target="tpu_custom_call" | custom-call | flops 2000000000 | bytes 4000000 | tf_op jit(solution)/shard_map/inputs/pallas_call | solution.py:288
  83.5 0.1 slice_reduce_fusion
  83.5 0.5 neg.3
  84.1 3.8 %all-to-all-done.2 = f32[4,256,128]{2,1,0:T(8,128)S(1)} async-done(((f32[4,256,128]{2,1,0:T(8,128)}), f32[4,256,128]{2,1,0:T(8,128)S(1)}, u32[]{:S(2)}, u32[]{:S(2)}) %all-to-all-start.2) | async-done | bytes 524320 | tf_op jit(solution)/shard_map/all_to_all | solution.py:335
  87.8 0.7 reduce_sum.18
  (6 shorter events, 0.0 us)
Async XLA Ops:
  1.3 1.1 %copy-start = (bf16[256,1280]{1,0:T(8,128)(2,1)S(1)}, bf16[256,1280]{1,0:T(8,128)(2,1)}, u32[]{:S(2)}) copy-start(bf16[256,1280]{1,0:T(8,128)(2,1)} %refs_6_.1) | copy-start | bytes 1966084
  2.4 0.8 copy-start.4
  3.2 0.7 copy-start.6
  3.9 0.7 copy-start.8
  4.6 16.7 %copy-start.1 = (bf16[256,1280]{1,0:T(8,128)(2,1)S(1)}, bf16[256,1280]{1,0:T(8,128)(2,1)}, u32[]{:S(2)}) copy-start(bf16[256,1280]{1,0:T(8,128)(2,1)} %refs_6_.1) | copy-start | bytes 1966084
  4.6 16.7 %copy-start.5 = (bf16[256,128]{1,0:T(8,128)(2,1)S(1)}, bf16[256,128]{1,0:T(8,128)(2,1)}, u32[]{:S(2)}) copy-start(bf16[256,128]{1,0:T(8,128)(2,1)} %refs_4_.3) | copy-start | bytes 196612
  4.6 16.7 %copy-start.7 = (f32[20,256]{1,0:T(8,128)S(1)}, f32[20,256]{1,0:T(8,128)}, u32[]{:S(2)}) copy-start(f32[20,256]{1,0:T(8,128)} %refs_2_.3) | copy-start | bytes 61444
  4.6 16.8 %copy-start.9 = (f32[20]{0:T(128)S(1)}, f32[20]{0:T(128)}, u32[]{:S(2)}) copy-start(f32[20]{0:T(128)} %refs_1_.1) | copy-start | bytes 244
  4.6 16.8 %copy-start.12 = (bf16[256,128]{1,0:T(8,128)(2,1)S(1)}, bf16[256,128]{1,0:T(8,128)(2,1)}, u32[]{:S(2)}) copy-start(bf16[256,128]{1,0:T(8,128)(2,1)} %refs_0_.3) | copy-start | bytes 196612
  6.4 4.6 %collective-permute-start = (f32[136,640]{1,0:T(8,128)S(1)}, f32[136,640]{1,0:T(8,128)S(1)}, u32[]{:S(2)}, u32[]{:S(2)}) collective-permute-start(f32[136,640]{1,0:T(8,128)S(1)} %get-tuple-element.18), channel_id=1, source_target_pairs={{0,4},{4,0},{1,5},{5,1},{2,6},{6,2},{3,7},{7,3},{8,12},{12,8},{9,1... | collective-permute-start | bytes 1044488 | tf_op jit(solution)/shard_map/ppermute | solution.py:310
  11.8 23.4 %all-to-all-start = ((f32[32,24,128]{2,1,0:T(8,128)}), f32[32,24,128]{2,1,0:T(8,128)S(1)}, u32[]{:S(2)}, u32[]{:S(2)}) async-start(f32[32,24,128]{2,1,0:T(8,128)} %bitcast.1), calls=%async_computation | async-start | bytes 786432 | tf_op jit(solution)/shard_map/all_to_all | solution.py:312
  21.4 1.1 %copy-start.10 = (bf16[256,1280]{1,0:T(8,128)(2,1)S(1)}, bf16[256,1280]{1,0:T(8,128)(2,1)}, u32[]{:S(2)}) copy-start(bf16[256,1280]{1,0:T(8,128)(2,1)} %refs_5_.3) | copy-start | bytes 1966084
  22.5 1.1 %copy-start.11 = (f32[1,20,64,128]{3,2,1,0:T(8,128)S(1)}, f32[1,20,64,128]{3,2,1,0:T(8,128)}, u32[]{:S(2)}) copy-start(f32[1,20,64,128]{3,2,1,0:T(8,128)} %param.14) | copy-start | bytes 1966084
  29.8 0.8 copy-start.2
  30.6 1.1 %copy-start.13 = (f32[256,1280]{1,0:T(8,128)}, f32[256,1280]{1,0:T(8,128)S(1)}, u32[]{:S(2)}) copy-start(f32[256,1280]{1,0:T(8,128)S(1)} %get-tuple-element.27.refs_2_) | copy-start | bytes 3932164
  31.7 1.1 %copy-start.15 = (f32[256,1280]{1,0:T(8,128)}, f32[256,1280]{1,0:T(8,128)S(1)}, u32[]{:S(2)}) copy-start(f32[256,1280]{1,0:T(8,128)S(1)} %get-tuple-element.28.refs_3_) | copy-start | bytes 3932164
  35.2 24.6 %copy-start.3 = (f32[128,1280]{1,0:T(8,128)S(1)}, f32[128,1280]{1,0:T(8,128)}, u32[]{:S(2)}) copy-start(f32[128,1280]{1,0:T(8,128)} %copy-done.2) | copy-start | bytes 1966084
  55.9 3.9 %collective-permute-start.1 = (f32[128,640]{1,0:T(8,128)S(1)}, f32[128,640]{1,0:T(8,128)S(1)}, u32[]{:S(2)}, u32[]{:S(2)}) collective-permute-start(f32[128,640]{1,0:T(8,128)S(1)} %get-tuple-element.21), channel_id=1, source_target_pairs={{0,4},{4,0},{1,5},{5,1},{2,6},{6,2},{3,7},{7,3},{8,12},{12,8},{9,1... | collective-permute-start | bytes 983048 | tf_op jit(solution)/shard_map/ppermute | solution.py:329
  75.5 12.3 %all-to-all-start.2 = ((f32[4,256,128]{2,1,0:T(8,128)}), f32[4,256,128]{2,1,0:T(8,128)S(1)}, u32[]{:S(2)}, u32[]{:S(2)}) async-start(f32[4,256,128]{2,1,0:T(8,128)} %get-tuple-element.29), calls=%async_computation.2 | async-start | bytes 1048576 | tf_op jit(solution)/shard_map/all_to_all | solution.py:335
  79.5 1.3 %copy-start.14 = (f32[256,1280]{1,0:T(8,128)S(1)}, f32[256,1280]{1,0:T(8,128)}, u32[]{:S(2)}) copy-start(f32[256,1280]{1,0:T(8,128)} %copy-done.13) | copy-start | bytes 3932164
  80.8 1.3 %copy-start.16 = (f32[256,1280]{1,0:T(8,128)S(1)}, f32[256,1280]{1,0:T(8,128)}, u32[]{:S(2)}) copy-start(f32[256,1280]{1,0:T(8,128)} %copy-done.15) | copy-start | bytes 3932164

commit v2 on v1

--- a/solution.py
+++ b/solution.py
@@ -85,27 +85,51 @@
     return elapsed, log_decay, steps
 
 
+def column_copies(sources, buffers, sems):
+    return [
+        [
+            pltpu.make_async_copy(
+                src.at[:, pl.ds(k * CHUNK, CHUNK)], dst.at[:, pl.ds(k * CHUNK, CHUNK)], sems.at[i, k]
+            )
+            for i, (src, dst) in enumerate(zip(sources, buffers))
+        ]
+        for k in range(STEPS)
+    ]
+
+
 def boundary_kernel(
-    reset_ref, core_ref, rate_ref, step_ref, c_ref, grad_ref, keep_ref, send_ref, pad_ref, all_ref
+    reset_ref, core_ref, rate_ref, step_hbm, c_hbm, grad_hbm,
+    keep_ref, send_ref,
+    pad_ref, all_ref, step_ref, c_ref, grad_ref, sems, small_sems,
 ):
+    get_steps = pltpu.make_async_copy(step_hbm, step_ref, small_sems.at[0])
+    get_c = pltpu.make_async_copy(c_hbm, c_ref, small_sems.at[1])
+    get_grad = column_copies([grad_hbm], [grad_ref], sems)
+    get_steps.start()
+    for copies in get_grad:
+        copies[0].start()
+    get_c.start()
     reset, core = reset_ref[0], core_ref[0]
+    get_steps.wait()
     elapsed, log_decay, _ = small_factors(rate_ref, step_ref, pad_ref, False)
     later = iota((SPAN, 128), 0) >= reset
     weight = packed(jnp.where(later, 0.0, jnp.exp(log_decay)))
     gain = jnp.where(reset >= SPAN, jnp.exp(log_decay[SPAN - 1 :, :]), 0.0)
     gain = packed(jnp.broadcast_to(gain, (8, 128)))
+    get_c.wait()
     for chunk in range(STEPS):
         cols = pl.ds(chunk * CHUNK, CHUNK)
         wide = spread(chunk)
-        weighted = dot(weight, wide, NN) * grad_ref[:, cols].astype(f32)
-        high, low = two_parts(weighted)
+        wide_weight = dot(weight, wide, NN)
+        all_ref[STATE:, cols] = dot(gain, wide, NN)
+        get_grad[chunk][0].wait()
+        high, low = two_parts(wide_weight * grad_ref[:, cols].astype(f32))
         all_ref[:STATE, cols] = dot(c_ref[...], high, TN) + dot(c_ref[...], low, TN)
-        all_ref[STATE:, cols] = dot(gain, wide, NN)
     keep_ref[...] = all_ref[:, pl.ds(pl.multiple_of(core * HALF, HALF), HALF)]
     send_ref[...] = all_ref[:, pl.ds(pl.multiple_of((1 - core) * HALF, HALF), HALF)]
 
 
-def combine_kernel(core_ref, keep_ref, got_ref, out_ref):
+def combine_kernel(core_ref, keep_ref, got_ref, out_ref, late_ref):
     first = core_ref[0] == 0
     upper = iota((STATE, 128), 0) & 7
 
@@ -113,6 +137,7 @@
         cols = slice(128 * t, 128 * t + 128)
         keep, got = keep_ref[:, cols], got_ref[:, cols]
         early, late = jnp.where(first, keep, got), jnp.where(first, got, keep)
+        late_ref[:, cols] = late
         early_gain, late_gain = early[STATE : STATE + 1], late[STATE : STATE + 1]
         return early[:STATE] + early_gain * late[:STATE], early_gain * late_gain
 
@@ -138,7 +163,7 @@
             run[i] = pieces[i] + tail[4 + i : 5 + i] * run[i]
 
 
-def return_kernel(core_ref, back_ref, keep_ref, got_ref, mine_ref, send_ref):
+def return_kernel(core_ref, back_ref, late_ref, mine_ref, send_ref):
     first = core_ref[0] == 0
     upper = iota((STATE, 128), 0) & 7
     for t in range(5):
@@ -149,31 +174,42 @@
             low = back_ref[0, :, 16:24, :].reshape(STATE, 128)
             high = back_ref[1, :, 16:24, :].reshape(STATE, 128)
             entering = jnp.where(upper < 4, low, pltpu.roll(high, 4, 0))
-        late = jnp.where(first, got_ref[:, cols], keep_ref[:, cols])
+        late = late_ref[:, cols]
         passed = late[:STATE] + late[STATE : STATE + 1] * entering
         mine_ref[:, cols] = jnp.where(first, passed, entering)
         send_ref[:, cols] = jnp.where(first, entering, passed)
 
 
 def local_kernel(
-    reset_ref,
-    rate_ref,
-    step_ref,
-    b_ref,
-    c_ref,
-    x_ref,
-    grad_ref,
-    state_ref,
-    inner_ref,
-    factor_ref,
-    high_ref,
-    low_ref,
-    inner_b_ref,
-    mate_ref,
-    rate_out_ref,
-    pad_ref,
-    pairs_ref,
+    reset_ref, rate_ref, step_hbm, b_hbm, c_hbm, x_hbm, grad_hbm, state_hbm,
+    inner_hbm, end_ref, high_ref, low_ref, inner_b_ref, mate_ref, rate_out_ref,
+    pad_ref, pairs_ref, step_ref, b_ref, c_ref, x_ref, grad_ref, state_ref, inner_ref,
+    sems, small_sems,
 ):
+    small = [
+        pltpu.make_async_copy(src, dst, small_sems.at[i])
+        for i, (src, dst) in enumerate(((step_hbm, step_ref), (b_hbm, b_ref), (c_hbm, c_ref)))
+    ]
+
+    def loads(chunk):
+        cols = pl.ds(pl.multiple_of(chunk * CHUNK, CHUNK), CHUNK)
+        return (
+            pltpu.make_async_copy(x_hbm.at[:, cols], x_ref.at[:, cols], sems.at[0, chunk]),
+            pltpu.make_async_copy(grad_hbm.at[:, cols], grad_ref.at[:, cols], sems.at[1, chunk]),
+            pltpu.make_async_copy(state_hbm.at[cols, :], state_ref.at[cols, :], sems.at[2, chunk]),
+        )
+
+    def store(chunk):
+        cols = pl.ds(pl.multiple_of(chunk * CHUNK, CHUNK), CHUNK)
+        return pltpu.make_async_copy(inner_ref.at[:, cols], inner_hbm.at[:, cols], sems.at[3, chunk])
+
+    for copy in small:
+        copy.start()
+    for chunk in range(STEPS):
+        for copy in loads(chunk):
+            copy.start()
+    for copy in small:
+        copy.wait()
     reset = reset_ref[0]
     elapsed, log_decay, steps = small_factors(rate_ref, step_ref, pad_ref, True)
     later = iota((SPAN, 128), 0) >= reset
@@ -185,6 +221,7 @@
     down = packed(steps * jnp.exp(-centred))
     end = jnp.where(later | no_reset, jnp.exp(last_log - log_decay), 0.0)
     end_steps = packed(steps * end)
+    end_ref[...] = end_steps
     elapsed_parts = packed(elapsed)
     rows = jnp.concatenate(
         [
@@ -208,6 +245,8 @@
         cols = pl.ds(pl.multiple_of(chunk * CHUNK, CHUNK), CHUNK)
         wide = spread(chunk)
         wide_rows = dot(rows, wide, NN)
+        for copy in loads(chunk):
+            copy.wait()
         x, grad = x_ref[:, cols].astype(f32), grad_ref[:, cols].astype(f32)
         wide_elapsed = dot(elapsed_parts, wide, NN)
         scaled_grad = dot(up, wide, NN) * grad
@@ -219,12 +258,12 @@
         plain = dot3(masked, grad_parts, NN)
         aged = dot3(masked, aged_parts, NN)
         inner_ref[:, cols] = wide_down * plain
+        store(chunk).start()
         inside = jnp.sum(scaled_x * (aged - wide_elapsed * plain), axis=0, keepdims=True)
         state = jnp.transpose(state_ref[cols, :])
         start = dot(c_start, aged_parts[0], TN) + dot(c_start, aged_parts[1], TN)
         entry = wide_rows[0:1] * jnp.sum(state * start, axis=0, keepdims=True)
         factor = dot(end_steps, wide, NN)
-        factor_ref[:, cols] = factor
         leaving = factor * x
         high, low = two_parts(leaving)
         high_ref[:, cols] = high
@@ -240,6 +279,8 @@
     lax.fori_loop(0, STEPS, step, 0)
     pairs = two_parts(jnp.where(joined, pairs_ref[...], 0.0))
     inner_b_ref[...] = dot(pairs[0], c, NN) + dot(pairs[1], c, NN)
+    for chunk in range(STEPS):
+        store(chunk).wait()
 
 
 def reduce_kernel(
@@ -259,86 +300,121 @@
         sums = three_parts(jnp.broadcast_to(sums, (8, CHUNK)))
         wide = spread(chunk)
         rate += dot(sums[0], wide, NT) + (dot(sums[1], wide, NT) + dot(sums[2], wide, NT))
-    for i in range(4):
-        grad_b_ref[i] = total
+    grad_b_ref[...] = total
     for i in range(64):
         rate_out_ref[i] = rate[0:1]
 
 
-def inputs_kernel(b_ref, all_ref, inner_ref, factor_ref, out_ref):
-    b = b_ref[...]
+def inputs_kernel(b_hbm, inner_hbm, all_ref, end_ref, out_ref, b_ref, inner_ref, sems, small_sems):
+    get_b = pltpu.make_async_copy(b_hbm, b_ref, small_sems.at[0])
+    get_inner = column_copies([inner_hbm], [inner_ref], sems)
+    get_b.start()
+    for copies in get_inner:
+        copies[0].start()
+    get_b.wait()
+    b, end = b_ref[...], end_ref[...]
     for chunk in range(STEPS):
         cols = pl.ds(chunk * CHUNK, CHUNK)
         high, low = two_parts(all_ref[:, cols])
-        product = dot(b, high, NN) + dot(b, low, NN)
-        out_ref[:, cols] = (inner_ref[:, cols] + factor_ref[:, cols] * product).astype(bf16)
+        product = dot(end, spread(chunk), NN) * (dot(b, high, NN) + dot(b, low, NN))
+        get_inner[chunk][0].wait()
+        out_ref[:, cols] = (inner_ref[:, cols] + product).astype(bf16)
 
 
 SMEM = pl.BlockSpec(memory_space=pltpu.SMEM)
 VMEM = pl.BlockSpec(memory_space=pltpu.VMEM)
 ANY = pl.BlockSpec(memory_space=pl.ANY)
-
-
-def call(
-    kernel, name, smem, args, outs, scratch=(), flops=1_000_000, size=1_000_000, after=(), grant=8
-):
+HBM = pl.BlockSpec(memory_space=pltpu.HBM)
+
+
+def in_hbm(a):
+    return pltpu.with_memory_space_constraint(a, pltpu.HBM)
+
+
+def call(kernel, name, scalars, far, near, outs, scratch=(), flops=1_000_000, after=(), grant=4):
+    count = len(scalars) + len(far) + len(near)
+
     def run(*refs):
-        kernel(*refs[: len(args)], *refs[len(args) + len(after) :])
+        kernel(*refs[:count], *refs[count + len(after) :])
 
     return pl.pallas_call(
         run,
         name=name,
-        in_specs=[SMEM] * smem + [VMEM] * (len(args) - smem) + [ANY] * len(after),
-        out_specs=[VMEM] * len(outs),
-        out_shape=[jax.ShapeDtypeStruct(shape, dtype) for shape, dtype in outs],
-        scratch_shapes=[pltpu.VMEM(shape, dtype) for shape, dtype in scratch],
-        cost_estimate=pl.CostEstimate(flops=flops, bytes_accessed=size, transcendentals=0),
+        in_specs=[SMEM] * len(scalars) + [HBM] * len(far) + [VMEM] * len(near) + [ANY] * len(after),
+        out_specs=[HBM if place == "far" else VMEM for _, _, place in outs],
+        out_shape=[
+            {"far": pltpu.HBM, "stored": pltpu.HBM, "near": pltpu.VMEM}[place](shape, dtype)
+            if place
+            else jax.ShapeDtypeStruct(shape, dtype)
+            for shape, dtype, place in outs
+        ],
+        scratch_shapes=list(scratch),
+        cost_estimate=pl.CostEstimate(flops=flops, bytes_accessed=1_000_000, transcendentals=0),
         compiler_params=pltpu.CompilerParams(vmem_limit_bytes=grant << 20),
-    )(*args, *after)
+    )(*scalars, *map(in_hbm, far), *near, *after)
 
 
 def body(inputs, time_step, decay_rate, input_map, output_map, output_grad, span_states, resets):
     core = lax.axis_index(CORE).astype(jnp.int32).reshape(1)
+    decay_rate = in_hbm(decay_rate)
     states = span_states.reshape(COLS, STATE)
     swap = [(0, 1), (1, 0)]
+    dma = pltpu.SemaphoreType.DMA
+    steps, maps = pltpu.VMEM((HEADS, SPAN), f32), pltpu.VMEM((SPAN, STATE), bf16)
+    wide, wide_f32 = pltpu.VMEM((SPAN, COLS), bf16), pltpu.VMEM((SPAN, COLS), f32)
+    padded = pltpu.VMEM((128, SPAN), f32)
     keep, send = call(
-        boundary_kernel, "boundary", 3,
-        (resets, core, decay_rate, time_step, output_map, output_grad),
-        [((STATE + 8, HALF), f32)] * 2,
-        [((128, SPAN), f32), ((STATE + 8, COLS), f32)],
+        boundary_kernel, "boundary",
+        (resets, core, decay_rate), (time_step, output_map, output_grad), (),
+        [((STATE + 8, HALF), f32, None)] * 2,
+        [padded, pltpu.VMEM((STATE + 8, COLS), f32), steps, maps, wide, dma((1, STEPS)), dma((2,))],
     )
     got = lax.ppermute(send, CORE, swap)
-    (pieces,) = call(combine_kernel, "combine", 1, (core, keep, got), [((2, 16, 24, 128), f32)])
+    pieces, late = call(
+        combine_kernel, "combine", (core,), (), (keep, got),
+        [((2, 16, 24, 128), f32, "near"), ((STATE + 8, HALF), f32, None)],
+    )
     received = lax.all_to_all(pieces.reshape(SHARES, 24, 128), CHIPS, 0, 0, tiled=True)
-    inner, factor, high, low, inner_b, mate, rate_local = call(
-        local_kernel, "local", 2,
-        (resets, decay_rate, time_step, input_map, output_map, inputs, output_grad, states),
+    inner, end, high, low, inner_b, mate, rate_local = call(
+        local_kernel, "local",
+        (resets, decay_rate),
+        (time_step, input_map, output_map, inputs, output_grad, states), (),
         [
-            ((SPAN, COLS), f32), ((SPAN, COLS), f32), ((SPAN, COLS), bf16), ((SPAN, COLS), bf16),
-            ((SPAN, STATE), f32), ((STATE, COLS), f32), ((8, 128), f32),
+            ((SPAN, COLS), f32, "far"), ((SPAN, 128), bf16, "stored"), ((SPAN, COLS), bf16, None),
+            ((SPAN, COLS), bf16, None), ((SPAN, STATE), f32, None), ((STATE, COLS), f32, None),
+            ((8, 128), f32, None),
         ],
-        [((128, SPAN), f32), ((SPAN, SPAN), f32)],
-        flops=6_000_000_000, size=8_000_000, after=(pieces,), grant=16,
-    )
-    (exclusive,) = call(scan_kernel, "carry", 0, (received,), [((SHARES, 24, 128), f32)], after=(rate_local,))
+        [
+            padded, pltpu.VMEM((SPAN, SPAN), f32), steps, maps, maps, wide, wide,
+            pltpu.VMEM((COLS, STATE), f32), wide_f32, dma((4, STEPS)), dma((3,)),
+        ],
+        flops=6_000_000_000, after=(pieces,), grant=12,
+    )
+    (exclusive,) = call(
+        scan_kernel, "carry", (), (), (received,), [((SHARES, 24, 128), f32, None)],
+        after=(rate_local,),
+    )
     back = lax.all_to_all(exclusive, CHIPS, 0, 0, tiled=True)
     mine, onward = call(
-        return_kernel, "spread", 1, (core, back.reshape(2, 16, 24, 128), keep, got),
-        [((STATE, HALF), f32)] * 2,
+        return_kernel, "spread", (core,), (), (back.reshape(2, 16, 24, 128), late),
+        [((STATE, HALF), f32, None)] * 2,
     )
     other = lax.ppermute(onward, CORE, swap)
     carried, grad_b, rate = call(
-        reduce_kernel, "reduce", 1, (core, mine, other, high, low, inner_b, mate, rate_local),
-        [((STATE, COLS), f32), ((4, SPAN, STATE), f32), ((64, 1, 128), f32)],
+        reduce_kernel, "reduce", (core,), (), (mine, other, high, low, inner_b, mate, rate_local),
+        [((STATE, COLS), f32, None), ((SPAN, STATE), f32, None), ((64, 1, 128), f32, "near")],
     )
     rates = lax.all_to_all(rate, SEQ, 0, 0, tiled=True)
-    grad_bs = lax.all_to_all(grad_b, "head", 0, 0, tiled=True)
+    near, far, across = (
+        lax.ppermute(grad_b, "head", [(i, (i + d) % 4) for i in range(4)]) for d in (1, 3, 2)
+    )
     (grad_inputs,) = call(
-        inputs_kernel, "inputs", 0, (input_map, carried, inner, factor), [((SPAN, COLS), bf16)],
-        flops=2_000_000_000, size=4_000_000,
+        inputs_kernel, "inputs", (), (input_map, inner), (carried, in_hbm(end)),
+        [((SPAN, COLS), bf16, None)],
+        [maps, wide_f32, dma((1, STEPS)), dma((1,))], flops=2_000_000_000,
     )
     grad_rate = -jnp.sum(rates[:, 0, :HEADS], axis=0)
-    return grad_inputs, jnp.sum(grad_bs, axis=0), grad_rate
+    return grad_inputs, (grad_b + across) + (near + far), grad_rate
 
 
 def solution(mesh):

time: 89.1 us -> 78.7 us (0.88)
  blocking collectives: 34.4 us -> 17.6 us
  local copies, waits for them, and re-layouts: 11.1 us -> 0 us
  Pallas kernels: 12.1 us -> 20.2 us
  starting transfers between devices: 19.5 us -> 26.2 us
  waiting for transfers between devices: 8.72 us -> 11.7 us
    all_to_all x1 -> x0, blocking collectives: 13.9 us -> none  [body(): rates = lax.all_to_all(rate, SEQ, 0, 0, tiled=True)]
    unnamed x34 -> x0, local copies, waits for them, and re-layouts: 11.1 us -> none
    pallas_call x7, Pallas kernels: 12.1 us -> 20.2 us  [call(): pl.pallas_call(run, name=name, in_specs=[SMEM] * len(scalars) + [HBM] * l...]
    ppermute x0 -> x3, starting transfers between devices: none -> 4.21 us  [body(): lax.ppermute(grad_b, 'head', [(i, (i + d) % 4) for i in range(4)])]
    all_to_all x1, blocking collectives: 20.5 us -> 17.6 us  [body(): back = lax.all_to_all(exclusive, CHIPS, 0, 0, tiled=True)]
    all_to_all x1, waiting for transfers between devices: 2.43 us -> 4.34 us  [body(): lax.all_to_all(pieces.reshape(SHARES, 24, 128), CHIPS, 0, 0, tiled=True)]
    all_to_all x1, starting transfers between devices: 4.03 us -> 5.54 us  [body(): rates = lax.all_to_all(rate, SEQ, 0, 0, tiled=True)]
    all_to_all x1, waiting for transfers between devices: 3.75 us -> 4.85 us  [body(): rates = lax.all_to_all(rate, SEQ, 0, 0, tiled=True)]
  transfers between devices with their start and end apart: 4 -> 7, of which waited for: 4 -> 4; matrix products, arithmetic and copies ran while one was open for 1% -> 1% of each run, Pallas kernels for 9% -> 18%
where the time goes in v2:
time: 78.7 us; the launch traced here: 78.3 us
  starting transfers between devices  26.2 us (33%)
  Pallas kernels  20.2 us (26%)
  blocking collectives  17.6 us (22%)
  waiting for transfers between devices  11.7 us (15%)
  between operations  1.34 us (2%)
  other arithmetic  1.28 us (2%)
    pallas_call x7, Pallas kernels, call(): pl.pallas_call(run, name=name, in_specs=[SMEM] * len(scalars) + [HBM] * l...  20.2 us
    all_to_all x1, blocking collectives, body(): back = lax.all_to_all(exclusive, CHIPS, 0, 0, tiled=True)  17.6 us
    all_to_all x1, starting transfers between devices, body(): lax.all_to_all(pieces.reshape(SHARES, 24, 128), CHIPS, 0, 0, tiled=True)  9.5 us
    all_to_all x1, starting transfers between devices, body(): rates = lax.all_to_all(rate, SEQ, 0, 0, tiled=True)  5.54 us
    all_to_all x1, waiting for transfers between devices, body(): rates = lax.all_to_all(rate, SEQ, 0, 0, tiled=True)  4.85 us
    all_to_all x1, waiting for transfers between devices, body(): lax.all_to_all(pieces.reshape(SHARES, 24, 128), CHIPS, 0, 0, tiled=True)  4.34 us
    ppermute x3, starting transfers between devices, body(): lax.ppermute(grad_b, 'head', [(i, (i + d) % 4) for i in range(4)])  4.21 us
    ppermute x1, starting transfers between devices, body(): other = lax.ppermute(onward, CORE, swap)  3.62 us
  transfers between devices with their start and end apart: 7, of which 4 were waited for; matrix products, arithmetic and copies ran while one was open for 1% of the time, Pallas kernels for 18%

profile of v2, /device:TPU:1, one launch (start us, length us, event | category | flops | bytes accessed | tf_op | source)
XLA Modules:
  0.0 78.3 jit_solution(9362960153485140633)
XLA Ops:
  1.3 3.6 %boundary.1 = (f32[136,640]{1,0:T(8,128)S(1)}, f32[136,640]{1,0:T(8,128)S(1)}) custom-call(s32[1]{0:T(128)S(6)} %copy.11.refs_0_, s32[1]{0:T(128)} %bitcast.1.refs_1_.refs_0_, f32[20]{0:T(128)} %refs_1_.1, f32[20,256]{1,0:T(8,128)} %refs_2_.3, bf16[256,128]{1,0:T(8,128)(2,1)} %refs_4_.3, bf16[256,1280]{1,0:T(8,128)(2,1)} %refs_6_.1), custom_call_target="tpu_custom_call" | custom-call | flops 1000000 | bytes 1000000 | tf_op jit(solution)/shard_map/boundary/pallas_call | solution.py:340
  4.9 3.3 %collective-permute-start = (f32[136,640]{1,0:T(8,128)S(1)}, f32[136,640]{1,0:T(8,128)S(1)}, u32[]{:S(2)}, u32[]{:S(2)}) collective-permute-start(f32[136,640]{1,0:T(8,128)S(1)} %get-tuple-element.20), channel_id=1, source_target_pairs={{0,4},{4,0},{1,5},{5,1},{2,6},{6,2},{3,7},{7,3},{8,12},{12,8},{9,1... | collective-permute-start | bytes 1044488 | tf_op jit(solution)/shard_map/ppermute | solution.py:372
  8.2 1.3 %collective-permute-done.refs_2_ = f32[136,640]{1,0:T(8,128)S(1)} collective-permute-done((f32[136,640]{1,0:T(8,128)S(1)}, f32[136,640]{1,0:T(8,128)S(1)}, u32[]{:S(2)}, u32[]{:S(2)}) %collective-permute-start) | collective-permute-done | bytes 348192 | tf_op jit(solution)/shard_map/ppermute | solution.py:372
  9.4 0.8 %combine.1 = (f32[2,16,24,128]{3,2,1,0:T(8,128)}, f32[136,640]{1,0:T(8,128)S(1)}) custom-call(s32[1]{0:T(128)} %bitcast.1.refs_1_.refs_0_, f32[136,640]{1,0:T(8,128)S(1)} %get-tuple-element.19.refs_1_, f32[136,640]{1,0:T(8,128)S(1)} %collective-permute-done.refs_2_), custom_call_target="tpu_custom_call" | custom-call | flops 1000000 | bytes 1000000 | tf_op jit(solution)/shard_map/combine/pallas_call | solution.py:340
  10.3 9.5 %all-to-all-start = ((f32[32,24,128]{2,1,0:T(8,128)}), f32[32,24,128]{2,1,0:T(8,128)S(1)}, u32[]{:S(2)}, u32[]{:S(2)}) async-start(f32[32,24,128]{2,1,0:T(8,128)} %bitcast.2), calls=%async_computation | async-start | bytes 786432 | tf_op jit(solution)/shard_map/all_to_all | solution.py:377
  19.8 9.5 %local.1 = (f32[256,1280]{1,0:T(8,128)}, bf16[256,128]{1,0:T(8,128)(2,1)}, bf16[256,1280]{1,0:T(8,128)(2,1)S(1)}, bf16[256,1280]{1,0:T(8,128)(2,1)S(1)}, f32[256...) custom-call(s32[1]{0:T(128)S(6)} %copy.11.refs_0_, f32[20]{0:T(128)} %refs_1_.1, ...), custom_call_target="tpu_custom_call" | custom-call | flops 6000000000 | bytes 1000000 | tf_op jit(solution)/shard_map/local/pallas_call | solution.py:340
  29.3 4.3 %all-to-all-done.refs_0_ = f32[32,24,128]{2,1,0:T(8,128)S(1)} async-done(((f32[32,24,128]{2,1,0:T(8,128)}), f32[32,24,128]{2,1,0:T(8,128)S(1)}, u32[]{:S(2)}, u32[]{:S(2)}) %all-to-all-start) | async-done | bytes 393248 | tf_op jit(solution)/shard_map/all_to_all | solution.py:377
  33.7 0.1 carry.1
  33.7 17.6 %all_to_all.15 = f32[32,24,128]{2,1,0:T(8,128)S(1)} all-to-all(f32[32,24,128]{2,1,0:T(8,128)S(1)} %carry.1), channel_id=1, replica_groups=mesh['seq_0'=8,'seq_1'=4,'seq_2'=2,'head'=4] {'seq_0','seq_1'}, dimensions={0} | all-to-all | bytes 786432 | tf_op jit(solution)/shard_map/all_to_all | solution.py:397
  51.3 0.1 spread.1
  51.4 3.6 %collective-permute-start.1 = (f32[128,640]{1,0:T(8,128)S(1)}, f32[128,640]{1,0:T(8,128)S(1)}, u32[]{:S(2)}, u32[]{:S(2)}) collective-permute-start(f32[128,640]{1,0:T(8,128)S(1)} %get-tuple-element.26), channel_id=1, source_target_pairs={{0,4},{4,0},{1,5},{5,1},{2,6},{6,2},{3,7},{7,3},{8,12},{12,8},{9,1... | collective-permute-start | bytes 983048 | tf_op jit(solution)/shard_map/ppermute | solution.py:402
  55.0 1.3 %collective-permute-done.1.refs_2_ = f32[128,640]{1,0:T(8,128)S(1)} collective-permute-done((f32[128,640]{1,0:T(8,128)S(1)}, f32[128,640]{1,0:T(8,128)S(1)}, u32[]{:S(2)}, u32[]{:S(2)}) %collective-permute-start.1) | collective-permute-done | bytes 327712 | tf_op jit(solution)/shard_map/ppermute | solution.py:402
  56.3 1.5 %reduce.2 = (f32[128,1280]{1,0:T(8,128)S(1)}, f32[256,128]{1,0:T(8,128)S(1)}, f32[64,1,128]{2,1,0:T(1,128)}) custom-call(s32[1]{0:T(128)} %bitcast.1.refs_1_.refs_0_, f32[128,640]{1,0:T(8,128)S(1)} %get-tuple-element.25.refs_1_, f32[128,640]{1,0:T(8,128)S(1)} %collective-permute-done.1.refs_2_, bf16[256,1280]{1,0:T(8,128)(2,1)S(1)} %get-tuple-element.27.refs_3_, ...), custom_call_target="tpu_custom_call" | custom-call | flops 1000000 | bytes 1000000 | tf_op jit(solution)/shard_map/reduce/pallas_call | solution.py:340
  57.8 2.5 %collective-permute-start.4 = (f32[256,128]{1,0:T(8,128)S(1)}, f32[256,128]{1,0:T(8,128)S(1)}, u32[]{:S(2)}, u32[]{:S(2)}) collective-permute-start(f32[256,128]{1,0:T(8,128)S(1)} %get-tuple-element.33), channel_id=1, source_target_pairs={{0,3},{1,0},{2,1},{3,2},{4,7},{5,4},{6,5},{7,6},{8,11},{9,8},{10,9... | collective-permute-start | bytes 393224 | tf_op jit(solution)/shard_map/ppermute | solution.py:409
  60.3 0.0 collective-permute-start.3
  60.3 1.7 %collective-permute-start.2 = (f32[256,128]{1,0:T(8,128)S(1)}, f32[256,128]{1,0:T(8,128)S(1)}, u32[]{:S(2)}, u32[]{:S(2)}) collective-permute-start(f32[256,128]{1,0:T(8,128)S(1)} %get-tuple-element.33), channel_id=1, source_target_pairs={{0,2},{1,3},{2,0},{3,1},{4,6},{5,7},{6,4},{7,5},{8,10},{9,11},{10,... | collective-permute-start | bytes 393224 | tf_op jit(solution)/shard_map/ppermute | solution.py:409
  62.1 5.5 %all-to-all-start.2 = ((f32[64,1,128]{2,1,0:T(1,128)}), f32[64,1,128]{2,1,0:T(1,128)S(1)}, u32[]{:S(2)}, u32[]{:S(2)}) async-start(f32[64,1,128]{2,1,0:T(1,128)} %get-tuple-element.34), calls=%async_computation.2 | async-start | bytes 65536 | tf_op jit(solution)/shard_map/all_to_all | solution.py:407
  67.6 4.6 %inputs.1 = bf16[256,1280]{1,0:T(8,128)(2,1)} custom-call(bf16[256,128]{1,0:T(8,128)(2,1)} %refs_0_.3, f32[256,1280]{1,0:T(8,128)} %get-tuple-element.22.refs_1_, f32[128,1280]{1,0:T(8,128)S(1)} %get-tuple-element.31.refs_2_, bf16[256,128]{1,0:T(8,128)(2,1)} %get-tuple-element.32.refs_3_), custom_call_target="tpu_custom_call" | custom-call | flops 2000000000 | bytes 1000000 | tf_op jit(solution)/shard_map/inputs/pallas_call | solution.py:340
  72.2 4.8 %all-to-all-done.2 = f32[64,1,128]{2,1,0:T(1,128)S(1)} async-done(((f32[64,1,128]{2,1,0:T(1,128)}), f32[64,1,128]{2,1,0:T(1,128)S(1)}, u32[]{:S(2)}, u32[]{:S(2)}) %all-to-all-start.2) | async-done | bytes 32800 | tf_op jit(solution)/shard_map/all_to_all | solution.py:407
  77.0 0.1 slice_reduce_fusion
  77.1 0.5 neg.3
  77.6 0.0 collective-permute-done.4
  77.6 0.0 collective-permute-done.3
  77.6 0.0 collective-permute-done.2
  77.6 0.7 add_add_fusion
Async XLA Ops:
  4.9 4.6 %collective-permute-start = (f32[136,640]{1,0:T(8,128)S(1)}, f32[136,640]{1,0:T(8,128)S(1)}, u32[]{:S(2)}, u32[]{:S(2)}) collective-permute-start(f32[136,640]{1,0:T(8,128)S(1)} %get-tuple-element.20), channel_id=1, source_target_pairs={{0,4},{4,0},{1,5},{5,1},{2,6},{6,2},{3,7},{7,3},{8,12},{12,8},{9,1... | collective-permute-start | bytes 1044488 | tf_op jit(solution)/shard_map/ppermute | solution.py:372
  10.3 23.4 %all-to-all-start = ((f32[32,24,128]{2,1,0:T(8,128)}), f32[32,24,128]{2,1,0:T(8,128)S(1)}, u32[]{:S(2)}, u32[]{:S(2)}) async-start(f32[32,24,128]{2,1,0:T(8,128)} %bitcast.2), calls=%async_computation | async-start | bytes 786432 | tf_op jit(solution)/shard_map/all_to_all | solution.py:377
  51.4 4.9 %collective-permute-start.1 = (f32[128,640]{1,0:T(8,128)S(1)}, f32[128,640]{1,0:T(8,128)S(1)}, u32[]{:S(2)}, u32[]{:S(2)}) collective-permute-start(f32[128,640]{1,0:T(8,128)S(1)} %get-tuple-element.26), channel_id=1, source_target_pairs={{0,4},{4,0},{1,5},{5,1},{2,6},{6,2},{3,7},{7,3},{8,12},{12,8},{9,1... | collective-permute-start | bytes 983048 | tf_op jit(solution)/shard_map/ppermute | solution.py:402
  57.8 19.8 %collective-permute-start.4 = (f32[256,128]{1,0:T(8,128)S(1)}, f32[256,128]{1,0:T(8,128)S(1)}, u32[]{:S(2)}, u32[]{:S(2)}) collective-permute-start(f32[256,128]{1,0:T(8,128)S(1)} %get-tuple-element.33), channel_id=1, source_target_pairs={{0,3},{1,0},{2,1},{3,2},{4,7},{5,4},{6,5},{7,6},{8,11},{9,8},{10,9... | collective-permute-start | bytes 393224 | tf_op jit(solution)/shard_map/ppermute | solution.py:409
  60.3 17.3 %collective-permute-start.3 = (f32[256,128]{1,0:T(8,128)S(1)}, f32[256,128]{1,0:T(8,128)S(1)}, u32[]{:S(2)}, u32[]{:S(2)}) collective-permute-start(f32[256,128]{1,0:T(8,128)S(1)} %get-tuple-element.33), channel_id=1, source_target_pairs={{0,1},{1,2},{2,3},{3,0},{4,5},{5,6},{6,7},{7,4},{8,9},{9,10},{10,1... | collective-permute-start | bytes 393224 | tf_op jit(solution)/shard_map/ppermute | solution.py:409
  60.3 17.3 %collective-permute-start.2 = (f32[256,128]{1,0:T(8,128)S(1)}, f32[256,128]{1,0:T(8,128)S(1)}, u32[]{:S(2)}, u32[]{:S(2)}) collective-permute-start(f32[256,128]{1,0:T(8,128)S(1)} %get-tuple-element.33), channel_id=1, source_target_pairs={{0,2},{1,3},{2,0},{3,1},{4,6},{5,7},{6,4},{7,5},{8,10},{9,11},{10,... | collective-permute-start | bytes 393224 | tf_op jit(solution)/shard_map/ppermute | solution.py:409
  62.1 15.0 %all-to-all-start.2 = ((f32[64,1,128]{2,1,0:T(1,128)}), f32[64,1,128]{2,1,0:T(1,128)S(1)}, u32[]{:S(2)}, u32[]{:S(2)}) async-start(f32[64,1,128]{2,1,0:T(1,128)} %get-tuple-element.34), calls=%async_computation.2 | async-start | bytes 65536 | tf_op jit(solution)/shard_map/all_to_all | solution.py:407
